TPU v7x, 32 devices: a whole 2x2x4 slice. The times are simulated.
32 devices in a mesh: groups: 2 (over y), tile: 8 (over z, x), feat: 2 (over core).
Axes of the slice: x: 2, y: 2, z: 4, core: 2. Of those that a mesh axis runs over, the one named last changes fastest.
Arguments:
- preacts: bfloat16 [3, 16384, 256], P(None, ('tile', 'feat'), 'groups'), parts along dimension 2, may hold values from -6 to 6
- targets: bfloat16 [3, 512, 1152], P(None, ('groups', 'tile', 'feat')), parts along dimension 1, may hold values from -4 to 4
- decoder: bfloat16 [16, 2, 12288, 2304], P(('groups', 'tile'), 'feat'), parts along dimension 0, may hold values from -0.02734375 to 0.02734375
- owner_list: int32 [16384, 6, 1], P(('tile', 'feat')), may hold values from 0 to 7; in each aligned block of 6144 rows (0 to 6143, 6144 to 12287, ..., all dimensions but the last counted through in order) at most 1536 rows name the same one
- tile_source: int32 [6], replicated, may hold values from 0 to 2, as said below
- tile_target: int32 [6], replicated, may hold values from 0 to 2, as said below
- row_order: int32 [4, 64], P('groups'), parts along dimension 0, may hold values from 0 to 63, each once within a row
Outputs:
- residual: float32 [3, 512, 1152], P(None, ('groups', 'tile', 'feat')), parts along dimension 1
- feature_grad: float32 [3, 16384, 256], P(None, ('tile', 'feat'), 'groups'), parts along dimension 2
There are 2 independent parts, one for each index of `groups`. A program takes and returns all parts, laid end to end along the dimension named above; an argument that names none is the same for every part. Nothing has to cross between parts.
Inputs may be any that keep to these rules, and one draw needn't show every extreme that they name: `owner_list`: among the 6144 rows of one device (features f with f // 1024 equal, all tiles), no owner is named more than 1536 times, and in some device one owner exactly 1536 times; every owner is named somewhere. `tile_source`: together with tile_target, every pair of layers s <= t appears exactly once. tile_target[k] >= tile_source[k]. `row_order`: each row is a permutation.
All inputs are finite; a program needn't handle non-finite values.
Results may differ from a plain program's by a relative error of at most 0.0027.
Values may be sent and summed in bfloat16 or wider, within the bound.
No kernel may reach another device: no remote copies, remote signals or barrier semaphores. Data moves between devices by JAX's collectives and lax.ppermute only.
A program may use at most 128 MiB of HBM per device.

v0:
```python
import jax
import jax.numpy as jnp
from jax import lax
from jax.sharding import PartitionSpec as P


def reorder(values, indices):
    leading = values.shape[:-1]
    blocks, block_span = indices.shape
    shaped = values.reshape(leading + (blocks, block_span))
    block_col = jnp.arange(blocks, dtype=jnp.int32)[:, None]
    return shaped[..., block_col, indices].reshape(values.shape)


def inverse_order(row_order):
    positions = lax.broadcasted_iota(jnp.int32, row_order.shape, 1)
    block_ids = lax.broadcasted_iota(jnp.int32, row_order.shape, 0)
    inverse = jnp.zeros(row_order.shape, jnp.int32)
    return inverse.at[block_ids, row_order].set(positions)


def on_device(preacts, targets, decoder, owner_list, tile_source, tile_target, row_order):
    owners = lax.axis_size("tile")
    layers, feat_dev, tokens = preacts.shape
    tile_count = tile_source.shape[0]
    slot_count = decoder.shape[2]
    capacity = slot_count // owners
    model_width = decoder.shape[3]
    inverse = inverse_order(row_order)
    active = jax.nn.relu(preacts.astype(jnp.float32)).astype(jnp.bfloat16)
    natural = reorder(active, inverse)
    picked = natural[tile_source]
    row_values = jnp.transpose(picked, (1, 0, 2)).reshape(feat_dev * tile_count, tokens)
    destination = owner_list.reshape(-1)
    count_rows = destination.shape[0]
    same_owner = destination[:, None] == destination[None, :]
    before = lax.broadcasted_iota(jnp.int32, (count_rows, count_rows), 0) < lax.broadcasted_iota(
        jnp.int32, (count_rows, count_rows), 1
    )
    slot_rank = jnp.sum((same_owner & before).astype(jnp.int32), axis=0)
    slot_of = destination * capacity + slot_rank
    slot_match = lax.broadcasted_iota(jnp.int32, (slot_count, count_rows), 0) == slot_of[None, :]
    packed = jnp.dot(
        slot_match.astype(jnp.bfloat16), row_values, preferred_element_type=jnp.float32
    ).astype(jnp.bfloat16)
    tile_of_row = lax.broadcasted_iota(jnp.int32, (feat_dev, tile_count), 1).reshape(-1)
    tile_slot = jnp.sum(jnp.where(slot_match, tile_of_row[None, :] + 1, 0), axis=1) - 1
    received, tile_recv = (
        lax.all_to_all(
            packed.reshape(owners, capacity, tokens),
            "tile",
            split_axis=0,
            concat_axis=0,
            tiled=True,
        ),
        lax.all_to_all(
            tile_slot.reshape(owners, capacity), "tile", split_axis=0, concat_axis=0, tiled=True
        ),
    )
    received = received.reshape(slot_count, tokens)
    tile_recv = tile_recv.reshape(slot_count)
    tile_ids = lax.broadcasted_iota(jnp.int32, (slot_count, tile_count), 1)
    target_slot = jnp.sum(
        jnp.where(tile_recv[:, None] == tile_ids, tile_target[None, :], 0), axis=1
    )
    occupied = tile_recv >= 0
    weights = decoder[0, 0]
    pieces = []
    for target_layer in range(layers):
        chosen = (occupied & (target_slot == target_layer))[:, None]
        masked = jnp.where(chosen, received, jnp.zeros_like(received))
        pieces.append(
            lax.dot_general(
                masked, weights, (((0,), (0,)), ((), ())), preferred_element_type=jnp.float32
            )
        )
    partial_value = jnp.stack(pieces).reshape(layers, 2 * tokens, model_width // 2)
    own_sums = lax.psum_scatter(partial_value, ("tile", "feat"), scatter_dimension=1, tiled=True)
    residual = own_sums - targets.astype(jnp.float32)
    spread = lax.all_gather(
        residual.astype(jnp.bfloat16), ("tile", "feat"), axis=1, tiled=True
    ).reshape(layers, tokens, model_width)
    slot_grad = jnp.zeros((slot_count, tokens), jnp.float32)
    for target_layer in range(layers):
        chosen = (occupied & (target_slot == target_layer))[:, None]
        product = lax.dot_general(
            weights,
            spread[target_layer],
            (((1,), (1,)), ((), ())),
            preferred_element_type=jnp.float32,
        )
        slot_grad = slot_grad + jnp.where(chosen, product, 0.0)
    returned = lax.all_to_all(
        slot_grad.reshape(owners, capacity, tokens), "tile", split_axis=0, concat_axis=0, tiled=True
    ).reshape(slot_count, tokens)
    row_grad = returned[slot_of].reshape(feat_dev, tile_count, tokens)
    layer_grad = jnp.stack(
        [
            jnp.sum(jnp.where((tile_source == source_layer)[None, :, None], row_grad, 0.0), axis=1)
            for source_layer in range(layers)
        ]
    )
    natural_pre = reorder(preacts, inverse)
    layer_grad = jnp.where(natural_pre > 0, layer_grad, 0.0)
    feature_grad = reorder(layer_grad, row_order)
    return (residual, feature_grad)


def solution(mesh):
    return jax.shard_map(
        on_device,
        mesh=mesh,
        in_specs=(
            P(None, ("tile", "feat"), "groups"),
            P(None, ("groups", "tile", "feat"), None),
            P(("groups", "tile"), "feat", None, None),
            P(("tile", "feat"), None, None),
            P(),
            P(),
            P("groups", None),
        ),
        out_specs=(P(None, ("groups", "tile", "feat"), None), P(None, ("tile", "feat"), "groups")),
        check_vma=False,
    )
```

profile of v0, /device:TPU:0, one launch (start us, length us, event | category | flops | bytes accessed | tf_op | source)
XLA Modules:
  0.0 728.4 jit_solution(1906964047460413758)
XLA Ops:
  8.6 34.1 %convert_reduce_fusion = s32[6144]{0:T(1024)S(1)} fusion(s32[6144]{0:T(1024)S(1)} %reshape.199), kind=kLoop, calls=%fused_computation.10 | loop fusion | flops 188737536 | bytes 49152 | tf_op jit(solution)/shard_map/reduce_sum | solution.py:40
  43.1 45.1 %select_reduce_fusion = s32[12288]{0:T(1024)S(1)} fusion(s32[6144]{0:T(1024)S(1)} %add.85, s32[6144]{0:T(1024)S(1)} %multiply_add_fusion), kind=kLoop, calls=%fused_computation.6 | loop fusion | flops 226480128 | bytes 98304 | tf_op jit(solution)/shard_map/reduce_sum | solution.py:47
  88.8 7.5 %all-to-all-start = ((s32[8,1,1536]{2,1,0:T(1,128)}), s32[8,1,1536]{2,1,0:T(1,128)S(1)}, u32[]{:S(2)}, u32[]{:S(2)}) async-start(s32[8,1,1536]{2,1,0:T(1,128)} %bitcast), calls=%async_computation | async-start | bytes 98304 | tf_op jit(solution)/shard_map/all_to_all | solution.py:56
  98.2 6.4 scatter_fusion
  107.1 1.9 gather_fusion.1
  109.1 2.5 copy.72
  113.0 55.0 %fusion.15 = bf16[12288,128]{1,0:T(8,128)(2,1)} fusion(bf16[6144,128]{1,0:T(8,128)(2,1)} %reshape.202, s32[6144]{0:T(1024)S(1)} %multiply_add_fusion), kind=kOutput, calls=%fused_computation.25 | convolution fusion | flops 19404423168 | bytes 4743168 | tf_op jit(solution)/shard_map/dot_general | solution.py:43
  168.1 6.1 all-to-all-start.1
  175.6 68.8 %all-to-all-done.1 = bf16[8,1536,128]{2,1,0:T(8,128)(2,1)S(1)} async-done(((bf16[8,1536,128]{2,1,0:T(8,128)(2,1)}), bf16[8,1536,128]{2,1,0:T(8,128)(2,1)S(1)}, u32[]{:S(2)}, u32[]{:S(2)}) %all-to-all-start.1) | async-done | bytes 3145760 | tf_op jit(solution)/shard_map/all_to_all | solution.py:49
  244.3 1.7 copy-done.2
  246.0 9.0 %broadcast_select_fusion.2 = (bf16[8,1536,128]{2,1,0:T(8,128)(2,1)S(1)}, bf16[8,1536,128]{2,1,0:T(8,128)(2,1)S(1)}, bf16[8,1536,128]{2,1,0:T(8,128)(2,1)}) fusion(bf16[8,1536,128]{2,1,0:T(8,128)(2,1)} %copy-done.2, pred[8,1536]{1,0:T(8,128)(4,1)S(1)} %get-tuple-element.24, pred[8,1536]{1,0:T(8,128)(4,1)S(1)} %get-tuple-element.35, ...), kind=kLoop, calls=%fused_computation.38 | loop fusion | flops 4718592 | bytes 12619776 | tf_op jit(solution)/shard_map/jit(_where)/select_n | solution.py:71
  255.0 21.1 %fusion.9 = f32[128,2304]{1,0:T(8,128)} fusion(bf16[12288,128]{1,0:T(8,128)(2,1)S(1)} %bitcast.94, bf16[1,1,12288,2304]{3,2,1,0:T(8,128)(2,1)} %param.9), kind=kOutput, calls=%fused_computation.19 | convolution fusion | flops 7247757312 | bytes 60948480 | tf_op jit(solution)/shard_map/dot_general | solution.py:73
  276.1 2.5 stack.26
  278.5 22.1 %fusion.11 = f32[128,2304]{1,0:T(8,128)} fusion(bf16[12288,128]{1,0:T(8,128)(2,1)} %bitcast.93, bf16[1,1,12288,2304]{3,2,1,0:T(8,128)(2,1)} %param.9), kind=kOutput, calls=%fused_computation.21 | convolution fusion | flops 7247757312 | bytes 60948480 | tf_op jit(solution)/shard_map/dot_general | solution.py:73
  300.6 2.5 stack.25
  303.1 21.0 %fusion.13 = f32[128,2304]{1,0:T(8,128)} fusion(bf16[12288,128]{1,0:T(8,128)(2,1)S(1)} %bitcast.92, bf16[1,1,12288,2304]{3,2,1,0:T(8,128)(2,1)} %param.9), kind=kOutput, calls=%fused_computation.23 | convolution fusion | flops 7247757312 | bytes 60948480 | tf_op jit(solution)/shard_map/dot_general | solution.py:73
  326.1 2.0 pad_maximum_fusion
  328.6 66.9 %reduce-scatter.2.cloned.1.call-done = f32[3,16,1152]{2,1,0:T(8,128)} async-done(((f32[3,256,1152]{2,1,0:T(8,128)}), f32[3,16,1152]{2,1,0:T(8,128)}) %reduce-scatter.2.cloned.1.call-update) | async-done | bytes 221200 | tf_op jit(solution)/shard_map/reduce_scatter | solution.py:78
  397.2 40.5 %all-gather.2.cloned.1.call-done = bf16[3,256,1152]{2,1,0:T(8,128)(2,1)} async-done(((bf16[3,16,1152]{2,1,0:T(8,128)(2,1)}), bf16[3,256,1152]{2,1,0:T(8,128)(2,1)}) %all-gather.2.cloned.1.call-update) | async-done | bytes 1769488 | tf_op jit(solution)/shard_map/all_gather | solution.py:80
  439.9 27.0 %fusion.28 = f32[128,12288]{1,0:T(8,128)} fusion(bf16[128,2304]{1,0:T(8,128)(2,1)S(1)} %squeeze.15, bf16[1,1,12288,2304]{3,2,1,0:T(8,128)(2,1)} %param.9, pred[12288]{0:T(1024)(128)(4,1)S(1)} %copy-done.14), kind=kOutput, calls=%fused_computation.30 | convolution fusion | flops 7249330176 | bytes 63516672 | tf_op jit(solution)/shard_map/dot_general | solution.py:86
  466.9 27.0 %fusion.25 = f32[128,12288]{1,0:T(8,128)} fusion(bf16[128,2304]{1,0:T(8,128)(2,1)S(1)} %squeeze.14, bf16[1,1,12288,2304]{3,2,1,0:T(8,128)(2,1)} %param.9, pred[12288]{0:T(1024)(128)(4,1)S(1)} %copy-done.13), kind=kOutput, calls=%fused_computation.29 | convolution fusion | flops 7249330176 | bytes 63516672 | tf_op jit(solution)/shard_map/dot_general | solution.py:86
  493.9 30.4 %fusion.22 = f32[128,12288]{1,0:T(8,128)} fusion(f32[128,12288]{1,0:T(8,128)} %fusion.28, f32[128,12288]{1,0:T(8,128)} %fusion.25, bf16[128,2304]{1,0:T(8,128)(2,1)S(1)} %squeeze.13, bf16[1,1,12288,2304]{3,2,1,0:T(8,128)(2,1)} %param.9, pred[12288]{0:T(1024)(128)(4,1)S(1)} %get-tuple-element.15), kind=kOutput, calls=%fused_computation.28 | convolution fusion | flops 7252475904 | bytes 76099584 | tf_op jit(solution)/shard_map/dot_general | solution.py:86
  524.3 6.0 copy.90
  530.4 4.9 all-to-all-start.2
  539.8 134.2 %all-to-all-done.2 = f32[8,1536,128]{1,2,0:T(8,128)} async-done(((f32[8,1536,128]{1,2,0:T(8,128)}), f32[8,1536,128]{1,2,0:T(8,128)}, u32[]{:S(2)}, u32[]{:S(2)}) %all-to-all-start.2) | async-done | bytes 6291488 | tf_op jit(solution)/shard_map/all_to_all | solution.py:93
  674.0 6.6 copy.76
  680.6 18.9 %gather_fusion.3 = f32[6144,128]{1,0:T(8,128)S(1)} fusion(f32[12288,128]{1,0:T(8,128)} %bitcast.89, s32[6144]{0:T(1024)S(1)} %broadcast_clamp_fusion), kind=kCustom, calls=%fused_computation.3 | custom fusion | bytes 6316032 | tf_op jit(solution)/shard_map/gather | solution.py:96
  699.4 2.3 reshape.207
  701.8 6.5 select_reduce_fusion.3
  712.4 3.2 maximum_select_fusion
  715.5 3.1 gather_fusion.4
  718.7 2.7 copy.83
  (96 shorter events, 24.3 us)
Async XLA Ops:
  7.2 89.2 %copy-start.8 = (bf16[3,1024,128]{2,1,0:T(8,128)(2,1)S(1)}, bf16[3,1024,128]{2,1,0:T(8,128)(2,1)}, u32[]{:S(2)}) copy-start(bf16[3,1024,128]{2,1,0:T(8,128)(2,1)} %param.7) | copy-start | bytes 2359300
  42.7 46.1 %copy-start.11 = (s32[6144]{0:T(1024)}, s32[6144]{0:T(1024)S(1)}, u32[]{:S(2)}) copy-start(s32[6144]{0:T(1024)S(1)} %convert_reduce_fusion) | copy-start | bytes 73732
  43.1 54.4 %copy-start.15 = (s32[2,64]{1,0:T(2,128)S(1)}, s32[2,64]{1,0:T(2,128)}, u32[]{:S(2)}) copy-start(s32[2,64]{1,0:T(2,128)} %param.13) | copy-start | bytes 1540
  88.8 79.2 %all-to-all-start = ((s32[8,1,1536]{2,1,0:T(1,128)}), s32[8,1,1536]{2,1,0:T(1,128)S(1)}, u32[]{:S(2)}, u32[]{:S(2)}) async-start(s32[8,1,1536]{2,1,0:T(1,128)} %bitcast), calls=%async_computation | async-start | bytes 98304 | tf_op jit(solution)/shard_map/all_to_all | solution.py:56
  96.6 1.5 copy-start.3
  104.7 2.3 copy-start
  104.7 2.4 copy-start.18
  168.1 6.4 copy-start.17
  168.1 76.3 %all-to-all-start.1 = ((bf16[8,1536,128]{2,1,0:T(8,128)(2,1)}), bf16[8,1536,128]{2,1,0:T(8,128)(2,1)S(1)}, u32[]{:S(2)}, u32[]{:S(2)}) async-start(bf16[8,1536,128]{2,1,0:T(8,128)(2,1)} %bitcast.100), calls=%async_computation.1 | async-start | bytes 6291456 | tf_op jit(solution)/shard_map/all_to_all | solution.py:49
  174.2 221.3 %reduce-scatter.2.cloned.1.call-start = ((), (), s32[]{:S(2)}) async-start(), calls=%async_computation.4 | async-start | bytes 3760128 | tf_op jit(solution)/shard_map/reduce_scatter | solution.py:78
  244.3 1.7 copy-start.2
  324.1 1.6 copy-start.5
  324.1 2.0 copy-start.6
  328.1 67.4 %copy-start.9 = (bf16[3,16,1152]{2,1,0:T(8,128)(2,1)S(1)}, bf16[3,16,1152]{2,1,0:T(8,128)(2,1)}, u32[]{:S(2)}) copy-start(bf16[3,16,1152]{2,1,0:T(8,128)(2,1)} %param.8) | copy-start | bytes 331780
  328.1 109.6 %all-gather.2.cloned.1.call-start = ((), (), s32[]{:S(2)}) async-start(), calls=%async_computation.5 | async-start | bytes 1880064 | tf_op jit(solution)/shard_map/all_gather | solution.py:80
  397.2 42.7 %copy-start.14 = (pred[12288]{0:T(1024)(128)(4,1)S(1)}, pred[12288]{0:T(1024)(128)(4,1)}, u32[]{:S(2)}) copy-start(pred[12288]{0:T(1024)(128)(4,1)} %get-tuple-element.32) | copy-start | bytes 36868
  439.9 27.1 %copy-start.13 = (pred[12288]{0:T(1024)(128)(4,1)S(1)}, pred[12288]{0:T(1024)(128)(4,1)}, u32[]{:S(2)}) copy-start(pred[12288]{0:T(1024)(128)(4,1)} %get-tuple-element.18) | copy-start | bytes 36868
  530.4 4.9 copy-start.4
  530.4 5.6 copy-start.1
  530.4 143.7 %all-to-all-start.2 = ((f32[8,1536,128]{1,2,0:T(8,128)}), f32[8,1536,128]{1,2,0:T(8,128)}, u32[]{:S(2)}, u32[]{:S(2)}) async-start(f32[8,1536,128]{1,2,0:T(8,128)} %bitcast.90), calls=%async_computation.3 | async-start | bytes 12582912 | tf_op jit(solution)/shard_map/all_to_all | solution.py:93
  535.2 2.4 copy-start.10
  535.3 3.0 copy-start.16
  535.3 3.1 copy-start.19
  535.3 3.1 copy-start.12
  708.3 4.1 copy-start.7
Sparse Core Ops, SparseCore 0:
  328.3 67.1 reduce-scatter.1
  398.4 39.2 all-gather.1
where the time goes:
time: 732 us; the launch traced here: 728 us
  waiting for transfers between devices  310 us (42%)
  matrix products  204 us (28%)
  other arithmetic  105 us (14%)
  local copies, waits for them, and re-layouts  75.2 us (10%)
  starting transfers between devices  19.2 us (3%)
  between operations  14.7 us (2%)
    all_to_all x1, waiting for transfers between devices, on_device(): lax.all_to_all(slot_grad.reshape(owners, capacity, tokens), 'tile', split...  134 us
    dot_general x3, matrix products, on_device(): lax.dot_general(weights, spread[target_layer], (((1,), (1,)), ((), ())),...  84.4 us
    all_to_all x1, waiting for transfers between devices, on_device(): lax.all_to_all(packed.reshape(owners, capacity, tokens), 'tile', split_ax...  68.8 us
    reduce_scatter x1, waiting for transfers between devices, on_device(): lax.psum_scatter(partial_value, ('tile', 'feat'), scatter_dimension=1, ti...  66.9 us
    dot_general x3, matrix products, on_device(): lax.dot_general(masked, weights, (((0,), (0,)), ((), ())), preferred_elem...  64.2 us
    dot_general x1, matrix products, on_device(): jnp.dot(slot_match.astype(jnp.bfloat16), row_values, preferred_element_ty...  55 us
    reduce_sum x1, other arithmetic, on_device(): jnp.sum(jnp.where(slot_match, tile_of_row[None, :] + 1, 0), axis=1) - 1  45.1 us
    all_gather x1, waiting for transfers between devices, on_device(): lax.all_gather(residual.astype(jnp.bfloat16), ('tile', 'feat'), axis=1, t...  40.5 us
  transfers between devices with their start and end apart: 5, of which 4 were waited for; matrix products, arithmetic and copies ran while one was open for 11% of the time, Pallas kernels for 0%

commit v1 on v0

--- a/solution.py
+++ b/solution.py
@@ -1,7 +1,20 @@
+import functools
+
 import jax
 import jax.numpy as jnp
 from jax import lax
+from jax.experimental import pallas as pl
+from jax.experimental.pallas import tpu as pltpu
 from jax.sharding import PartitionSpec as P
+
+
+META = 16
+UNROLL = 8
+NCOL = 768
+SPLIT = 2
+SEND_ORDER = (4, 1, 2, 3, 5, 6, 7)
+FORWARD_RUNS = ((0,), (1, 2, 3), (4, 5), (6,), (7,))
+BACKWARD_RUNS = ((4,), (5,), (6, 7), (3, 2, 1, 0))
 
 
 def reorder(values, indices):
@@ -19,7 +32,7 @@
     return inverse.at[block_ids, row_order].set(positions)
 
 
-def on_device(preacts, targets, decoder, owner_list, tile_source, tile_target, row_order):
+def on_device_general(preacts, targets, decoder, owner_list, tile_source, tile_target, row_order):
     owners = lax.axis_size("tile")
     layers, feat_dev, tokens = preacts.shape
     tile_count = tile_source.shape[0]
@@ -106,6 +119,435 @@
     return (residual, feature_grad)
 
 
+def vmem(limit=60):
+    return pltpu.CompilerParams(vmem_limit_bytes=limit * 2**20)
+
+
+def full(shape):
+    return pl.BlockSpec(shape, lambda *_: (0,) * len(shape))
+
+
+def pack_kernel(slot_sm, src_sm, pre_ref, perm_ref, meta_ref, *refs):
+    outs, (nat, packed) = refs[:-2], refs[-2:]
+    layers, feats, _ = pre_ref.shape
+    tiles = src_sm.shape[0]
+    capacity = packed.shape[0] // len(outs)
+    for s in range(layers):
+        active = jnp.maximum(pre_ref[s].astype(jnp.float32), 0.0).astype(jnp.bfloat16)
+        nat[pl.ds(s * feats, feats), :] = jnp.dot(
+            active, perm_ref[...], preferred_element_type=jnp.float32
+        )
+    bases = [src_sm[k] * feats for k in range(tiles)]
+
+    def step(i, carry):
+        for j in range(UNROLL):
+            f = i * UNROLL + j
+            for k in range(tiles):
+                slot = slot_sm[f * tiles + k]
+                packed[pl.ds(slot, 1), :] = nat[pl.ds(bases[k] + f, 1), :]
+        return carry
+
+    lax.fori_loop(0, feats // UNROLL, step, 0)
+    for d, out_ref in enumerate(outs):
+        out_ref[:capacity, :] = packed[d * capacity : (d + 1) * capacity, :].astype(jnp.bfloat16)
+        out_ref[capacity:, :] = meta_ref[d]
+
+
+def slot_targets(meta, tgt_sm):
+    values = meta.astype(jnp.float32)
+    target = jnp.full(values.shape, -1.0, jnp.float32)
+    for k in range(tgt_sm.shape[0]):
+        target = jnp.where(values == float(k + 1), tgt_sm[k].astype(jnp.float32), target)
+    return target
+
+
+def forward_kernel(count, first, last, tgt_sm, seq_sm, me_sm, half_sm, *refs):
+    recv_refs, w_ref, refs = refs[:count], refs[count], refs[count + 1 :]
+    if not first:
+        before_ref, refs = refs[0], refs[1:]
+    outs, (acc, lhs, goal, stage) = refs[:-4], refs[-4:]
+    i = pl.program_id(0)
+    depth, width = w_ref.shape
+    capacity = depth * SPLIT
+    tokens = recv_refs[0].shape[1]
+    layers = lhs.shape[0] // tokens
+    groups = depth // 128
+    for n in range(count * SPLIT):
+
+        @pl.when(i == n)
+        def _():
+            recv_ref, first_row = recv_refs[n // SPLIT], n % SPLIT * groups
+            target = slot_targets(recv_ref[capacity:, :], tgt_sm)
+            goal[:groups, :] = target[first_row : first_row + groups, :]
+            stage[...] = recv_ref[first_row * 128 : (first_row + groups) * 128, :]
+
+    for j in range(groups):
+        span = slice(j * 128, (j + 1) * 128)
+        acts = stage[span, :].astype(jnp.float32).T
+        for t in range(layers):
+            lhs[t * tokens : (t + 1) * tokens, span] = jnp.where(
+                goal[j : j + 1, :] == float(t), acts, 0.0
+            ).astype(jnp.bfloat16)
+
+    @pl.when(i == 0)
+    def _():
+        acc[...] = jnp.zeros_like(acc) if first else before_ref[...]
+
+    for n in range(width // NCOL):
+        cols = slice(n * NCOL, (n + 1) * NCOL)
+        acc[:, cols] += jnp.dot(lhs[...], w_ref[:, cols], preferred_element_type=jnp.float32)
+
+    @pl.when(i == count * SPLIT - 1)
+    def _():
+        if not last:
+            outs[0][...] = acc[...]
+            return
+        owners = outs[0].shape[0]
+        for d in range(owners):
+            for t in range(layers):
+                for side, half in enumerate((half_sm[0], 1 - half_sm[0])):
+                    place = pl.multiple_of(t * tokens + (me_sm[0] ^ d) * 16 + half * 8, 8)
+                    values = acc[pl.ds(place, 8), :]
+                    if t < layers - 1:
+                        outs[2 * side][d, t * 8 : (t + 1) * 8, :] = values
+                    else:
+                        outs[2 * side + 1][d] = values
+
+
+def backward_kernel(count, first, tgt_sm, seq_sm, me_sm, *all_refs):
+    refs = all_refs
+    meta_refs, w_ref, refs = refs[:count], refs[count], refs[count + 1 : -2]
+    goal, stage = all_refs[-2:]
+    i = pl.program_id(0)
+    if first:
+        mine_ref, other_ref, place_ref = refs[:3]
+        outs, spread = refs[3:-1], refs[-1]
+        half = mine_ref.shape[0]
+
+        @pl.when(i == 0)
+        def _():
+            spread[...] = (
+                jnp.dot(place_ref[:, :half], mine_ref[...], preferred_element_type=jnp.float32)
+                + jnp.dot(place_ref[:, half:], other_ref[...], preferred_element_type=jnp.float32)
+            ).astype(jnp.bfloat16)
+
+    else:
+        spread, outs = refs[0], refs[1:]
+    depth = w_ref.shape[0]
+    tokens = outs[0].shape[1]
+    layers = spread.shape[0] // tokens
+    groups = depth // 128
+    for n in range(count * SPLIT):
+
+        @pl.when(i == n)
+        def _():
+            first_row = n % SPLIT * groups
+            target = slot_targets(meta_refs[n // SPLIT][...], tgt_sm)
+            goal[:groups, :] = target[first_row : first_row + groups, :]
+
+    for j in range(depth // 256):
+        grads = lax.dot_general(
+            spread[...],
+            w_ref[j * 256 : (j + 1) * 256, :],
+            (((1,), (1,)), ((), ())),
+            preferred_element_type=jnp.float32,
+        )
+        for h in range(2):
+            row = goal[2 * j + h : 2 * j + h + 1, :]
+            chosen = jnp.zeros((tokens, 128), jnp.float32)
+            for t in range(layers):
+                part = grads[t * tokens : (t + 1) * tokens, h * 128 : (h + 1) * 128]
+                chosen = jnp.where(row == float(t), part, chosen)
+            begin = j * 256 + h * 128
+            stage[begin : begin + 128, :] = chosen.T.astype(jnp.bfloat16)
+    for n in range(count * SPLIT):
+
+        @pl.when(i == n)
+        def _():
+            outs[n // SPLIT][n % SPLIT * depth : (n % SPLIT + 1) * depth, :] = stage[...]
+
+
+def unpack_kernel(slot_sm, order_sm, *refs):
+    backs, (pre_ref, out_ref, rows) = refs[:-3], refs[-3:]
+    layers, feats, _ = pre_ref.shape
+    tiles = order_sm.shape[0]
+    capacity = rows.shape[0] // len(backs)
+    for d, back_ref in enumerate(backs):
+        rows[d * capacity : (d + 1) * capacity, :] = back_ref[...].astype(jnp.float32)
+    order = [order_sm[k] for k in range(tiles)]
+
+    def step(i, carry):
+        for j in range(UNROLL):
+            f = i * UNROLL + j
+            k = 0
+            for s in range(layers):
+                total = None
+                for _ in range(layers - s):
+                    row = rows[pl.ds(slot_sm[f * tiles + order[k]], 1), :]
+                    total = row if total is None else total + row
+                    k += 1
+                out_ref[s, pl.ds(f, 1), :] = total
+        return carry
+
+    lax.fori_loop(0, feats // UNROLL, step, 0)
+    for s in range(layers):
+        out_ref[s] = jnp.where(pre_ref[s].astype(jnp.float32) > 0, out_ref[s], 0.0)
+
+
+def slot_plan(owner_list, tile_count, owners, capacity):
+    count = owner_list.size
+    blocks = count // 128
+    dest = owner_list.reshape(blocks, 128)
+    same = dest[None] == lax.broadcasted_iota(jnp.int32, (owners, 1, 1), 0)
+    ones = same.astype(jnp.bfloat16)
+    lane = lax.broadcasted_iota(jnp.int32, (128, 128), 0) < lax.broadcasted_iota(
+        jnp.int32, (128, 128), 1
+    )
+    ahead = lax.broadcasted_iota(jnp.int32, (blocks, blocks), 0) < lax.broadcasted_iota(
+        jnp.int32, (blocks, blocks), 1
+    )
+    within = jnp.einsum(
+        "pbi,ij->pbj", ones, lane.astype(jnp.bfloat16), preferred_element_type=jnp.float32
+    )
+    totals = jnp.sum(ones, axis=2, dtype=jnp.float32).astype(jnp.bfloat16)
+    base = jnp.dot(totals, ahead.astype(jnp.bfloat16), preferred_element_type=jnp.float32)
+    rank = jnp.sum(jnp.where(same, within + base[:, :, None], 0.0), axis=0).astype(jnp.int32)
+    slot = (dest * capacity + rank).reshape(1, count)
+    slots = owners * capacity
+    tile = lax.broadcasted_iota(jnp.int32, (1, count), 1) % tile_count
+    high = lax.broadcasted_iota(jnp.int32, (slots // 128, 1), 0) == slot // 128
+    low = lax.broadcasted_iota(jnp.int32, (128, 1), 0) == slot % 128
+    meta = lax.dot_general(
+        jnp.where(high, (tile + 1).astype(jnp.bfloat16), 0),
+        low.astype(jnp.bfloat16),
+        (((1,), (1,)), ((), ())),
+        preferred_element_type=jnp.float32,
+    )
+    meta = meta.reshape(owners, capacity // 128, 128).astype(jnp.bfloat16)
+    meta = jnp.pad(meta, ((0, 0), (0, META - capacity // 128), (0, 0)))
+    return slot.reshape(count), meta
+
+
+def on_device_fast(*args):
+    return fast_step(*args)
+
+
+def fast_step(preacts, targets, decoder, owner_list, tile_source, tile_target, row_order):
+    owners = lax.axis_size("tile")
+    my_half = lax.axis_index("feat")
+    layers, feats, tokens = preacts.shape
+    tiles = tile_source.shape[0]
+    slots, width = decoder.shape[2:]
+    capacity = slots // owners
+    rows = layers * 8
+    weights = decoder.reshape(slots, width)
+    bf16, f32, i32 = jnp.bfloat16, jnp.float32, jnp.int32
+
+    me = lax.axis_index("tile")
+    slot, meta = slot_plan(owner_list ^ me, tiles, owners, capacity)
+    me_id = jnp.reshape(me, (1,)).astype(i32)
+    half_id = jnp.reshape(my_half, (1,)).astype(i32)
+    block_of = lax.broadcasted_iota(i32, row_order.shape, 0) * row_order.shape[1]
+    token_of = (row_order + block_of).reshape(tokens)
+    perm = (token_of[:, None] == lax.broadcasted_iota(i32, (1, tokens), 1)).astype(bf16)
+    index = lax.broadcasted_iota(i32, (1, layers * tokens), 1)
+    side = jnp.where(index // (owners * rows) == 0, my_half, 1 - my_half)
+    held = (index % (owners * rows)) // rows * 16 + side * 8 + index % 8
+    held_layer = index % rows // 8
+    wanted = jnp.tile(token_of, layers)[:, None]
+    wanted_layer = lax.broadcasted_iota(i32, (layers * tokens, 1), 0) // tokens
+    place = ((held == wanted) & (held_layer == wanted_layer)).astype(bf16)
+    tile_ids = jnp.arange(tiles, dtype=i32)
+    earlier = (tile_source[None, :] < tile_source[:, None]) | (
+        (tile_source[None, :] == tile_source[:, None]) & (tile_ids[None, :] < tile_ids[:, None])
+    )
+    position = jnp.sum(earlier.astype(i32), axis=1)
+    order = jnp.sum(
+        jnp.where(position[None, :] == tile_ids[:, None], tile_ids[None, :], 0), axis=1
+    ).astype(i32)
+
+    def to_peer(d, block):
+        return lax.ppermute(block, "tile", [(q, q ^ d) for q in range(owners)])
+
+    mirror = owners // 2
+    near = range(1, mirror)
+    block = jax.ShapeDtypeStruct((capacity + META, tokens), bf16)
+    packed = pl.pallas_call(
+        pack_kernel,
+        out_shape=[block] * owners,
+        grid_spec=pltpu.PrefetchScalarGridSpec(
+            num_scalar_prefetch=2,
+            grid=(1,),
+            in_specs=[full(preacts.shape), full(perm.shape), full(meta.shape)],
+            out_specs=[full(block.shape)] * owners,
+            scratch_shapes=[
+                pltpu.VMEM((layers * feats, tokens), f32),
+                pltpu.VMEM((slots, tokens), f32),
+            ],
+        ),
+        compiler_params=vmem(32),
+    )(slot, tile_source, preacts, perm, meta)
+    received = list(packed)
+    for d in SEND_ORDER:
+        received[d] = to_peer(d, packed[d])
+
+    def cost(count):
+        return pl.CostEstimate(
+            flops=2 * layers * tokens * count * capacity * width,
+            bytes_accessed=2 * count * capacity * width,
+            transcendentals=0,
+        )
+
+    weight_spec = pl.BlockSpec(
+        (capacity // SPLIT, width),
+        lambda i, tgt, seq, me, *_: ((me[0] ^ seq[i // SPLIT]) * SPLIT + i % SPLIT, 0),
+    )
+    whole = pl.BlockSpec(memory_space=pltpu.VMEM)
+
+    def forward(run, before, last):
+        first, count = before is None, len(run)
+        if last:
+            outs = [
+                jax.ShapeDtypeStruct((owners, rows - 8, width), f32),
+                jax.ShapeDtypeStruct((owners, 8, width), f32),
+            ] * 2
+        else:
+            outs = [jax.ShapeDtypeStruct((layers * tokens, width), f32)]
+        sums = [] if first else [before]
+        return pl.pallas_call(
+            functools.partial(forward_kernel, count, first, last),
+            out_shape=outs,
+            grid_spec=pltpu.PrefetchScalarGridSpec(
+                num_scalar_prefetch=4,
+                grid=(count * SPLIT,),
+                in_specs=[whole] * count + [weight_spec] + [whole] * len(sums),
+                out_specs=[whole] * len(outs),
+                scratch_shapes=[
+                    pltpu.VMEM((layers * tokens, width), f32),
+                    pltpu.VMEM((layers * tokens, capacity // SPLIT), bf16),
+                    pltpu.VMEM((META, 128), f32),
+                    pltpu.VMEM((capacity // SPLIT, tokens), bf16),
+                ],
+            ),
+            compiler_params=vmem(28),
+            cost_estimate=cost(count),
+        )(
+            tile_target,
+            jnp.array(run, i32),
+            me_id,
+            half_id,
+            *[received[d] for d in run],
+            weights,
+            *sums,
+        )
+
+    value = None
+    for number, run in enumerate(FORWARD_RUNS):
+        last = number == len(FORWARD_RUNS) - 1
+        value = forward(run, value, last)
+        if not last:
+            value = value[0]
+
+    swap = [(0, 1), (1, 0)]
+    keep_most, keep_last, send_most, send_last = value
+    got_last = lax.ppermute(send_last, "feat", swap)
+    got_most = lax.ppermute(send_most, "feat", swap)
+    last_sum = keep_last + got_last
+    across = to_peer(mirror, last_sum[mirror:])
+    most_sum = (keep_most + got_most).reshape(2, mirror, rows - 8, width)
+    pair = most_sum[:, 0]
+    for d in near:
+        pair = pair + to_peer(d, most_sum[:, d])
+    last_sum = last_sum[:mirror] + across
+    own_last = last_sum[0]
+    for d in near:
+        own_last = own_last + to_peer(d, last_sum[d])
+    own_most = pair[0] + to_peer(mirror, pair[1])
+    residual = jnp.concatenate([own_most, own_last]) - targets.astype(f32).reshape(rows, width)
+    mine = lax.all_to_all(
+        jnp.broadcast_to(residual.astype(bf16)[None], (owners, rows, width)),
+        "tile",
+        split_axis=0,
+        concat_axis=0,
+        tiled=True,
+    ).reshape(owners * rows, width)
+    other = lax.ppermute(mine, "feat", swap)
+
+    grad_block = jax.ShapeDtypeStruct((capacity, tokens), bf16)
+    spread_type = jax.ShapeDtypeStruct((layers * tokens, width), bf16)
+    meta_spec = pl.BlockSpec((META, tokens), lambda *_: (capacity // META, 0))
+
+    def backward(run, known):
+        first, count = len(known) > 1, len(run)
+        outs = [grad_block] * count + ([spread_type] if first else [])
+        return pl.pallas_call(
+            functools.partial(backward_kernel, count, first),
+            out_shape=outs,
+            grid_spec=pltpu.PrefetchScalarGridSpec(
+                num_scalar_prefetch=3,
+                grid=(count * SPLIT,),
+                in_specs=[meta_spec] * count + [weight_spec] + [whole] * len(known),
+                out_specs=[whole] * len(outs),
+                scratch_shapes=[
+                    pltpu.VMEM((META, 128), f32),
+                    pltpu.VMEM((capacity // SPLIT, tokens), bf16),
+                ],
+            ),
+            compiler_params=vmem(28),
+            cost_estimate=cost(count),
+        )(
+            tile_target,
+            jnp.array(run, i32),
+            me_id,
+            *[received[d] for d in run],
+            weights,
+            *known,
+        )
+
+    returned = [None] * owners
+    known = (mine, other, place)
+    for run in BACKWARD_RUNS:
+        grads = backward(run, known)
+        if len(known) > 1:
+            known = (grads[len(run)],)
+        for d, grad in zip(run, grads):
+            returned[d] = to_peer(d, grad) if d else grad
+
+    feature_grad = pl.pallas_call(
+        unpack_kernel,
+        out_shape=jax.ShapeDtypeStruct(preacts.shape, f32),
+        grid_spec=pltpu.PrefetchScalarGridSpec(
+            num_scalar_prefetch=2,
+            grid=(1,),
+            in_specs=[full(grad_block.shape)] * owners + [full(preacts.shape)],
+            out_specs=full(preacts.shape),
+            scratch_shapes=[pltpu.VMEM((slots, tokens), f32)],
+        ),
+        compiler_params=vmem(32),
+    )(slot, order, *returned, preacts)
+    return residual.reshape(targets.shape), feature_grad
+
+
+def on_device(preacts, targets, decoder, owner_list, tile_source, tile_target, row_order):
+    args = (preacts, targets, decoder, owner_list, tile_source, tile_target, row_order)
+    owners, halves = lax.axis_size("tile"), lax.axis_size("feat")
+    layers, feat_dev, tokens = preacts.shape
+    tile_count = tile_source.shape[0]
+    slot_count, model_width = decoder.shape[2:]
+    fits = (
+        tokens == 128
+        and halves == 2
+        and tokens == 8 * owners * halves
+        and slot_count % (owners * 256) == 0
+        and slot_count <= owners * META * 128
+        and (feat_dev * tile_count) % 128 == 0
+        and feat_dev % UNROLL == 0
+        and tile_count * 2 == layers * (layers + 1)
+        and model_width % 256 == 0
+    )
+    return (on_device_fast if fits else on_device_general)(*args)
+
+
 def solution(mesh):
     return jax.shard_map(
         on_device,

time: 732 us -> 279 us (0.38)
  matrix products: 204 us -> 1.06 us
  waiting for transfers between devices: 310 us -> 108 us
  Pallas kernels: 0 us -> 104 us
  other arithmetic: 105 us -> 6.68 us
  local copies, waits for them, and re-layouts: 75.2 us -> 6.95 us
  starting transfers between devices: 19.2 us -> 50.2 us
  between operations: 14.7 us -> 1.05 us
    dot_general x7 -> x3, matrix products: 204 us -> 1.06 us  [the longest x1 0.74 us: slot_plan(): lax.dot_general(jnp.where(high, (tile + 1).astype(jnp.bfloat16), 0), low....]
    all_to_all x3 -> x1, waiting for transfers between devices: 203 us -> 22.1 us  [fast_step(): lax.all_to_all(jnp.broadcast_to(residual.astype(bf16)[None], (owners, row...]
    pallas_call x0 -> x11, Pallas kernels: none -> 104 us  [the longest x5 45.1 us: forward(): pl.pallas_call(functools.partial(forward_kernel, count, first, last), out...]
    ppermute x0 -> x25, waiting for transfers between devices: none -> 86 us  [the longest x22 84.2 us: to_peer(): return lax.ppermute(block, 'tile', [(q, q ^ d) for q in range(owners)])]
    reduce_sum x4 -> x3, other arithmetic: 85.9 us -> 0.43 us  [the longest x1 0.18 us: fast_step(): position = jnp.sum(earlier.astype(i32), axis=1)]
    reduce_scatter x1 -> x0, waiting for transfers between devices: 66.9 us -> none  [on_device(): lax.psum_scatter(partial_value, ('tile', 'feat'), scatter_dimension=1, ti...]
    ppermute x0 -> x25, starting transfers between devices: none -> 45.5 us  [the longest x22 45 us: to_peer(): return lax.ppermute(block, 'tile', [(q, q ^ d) for q in range(owners)])]
    all_gather x1 -> x0, waiting for transfers between devices: 40.5 us -> none  [on_device(): lax.all_gather(residual.astype(jnp.bfloat16), ('tile', 'feat'), axis=1, t...]
  transfers between devices with their start and end apart: 5 -> 26, of which waited for: 4 -> 15; matrix products, arithmetic and copies ran while one was open for 11% -> 2% of each run, Pallas kernels for 0% -> 22%
where the time goes in v1:
time: 279 us; the launch traced here: 278 us
  waiting for transfers between devices  108 us (39%)
  Pallas kernels  104 us (37%)
  starting transfers between devices  50.2 us (18%)
  local copies, waits for them, and re-layouts  6.95 us (2%)
  other arithmetic  6.68 us (2%)
    ppermute x22, waiting for transfers between devices, to_peer(): return lax.ppermute(block, 'tile', [(q, q ^ d) for q in range(owners)])  84.2 us
    pallas_call x5, Pallas kernels, forward(): pl.pallas_call(functools.partial(forward_kernel, count, first, last), out...  45.1 us
    ppermute x22, starting transfers between devices, to_peer(): return lax.ppermute(block, 'tile', [(q, q ^ d) for q in range(owners)])  45 us
    pallas_call x4, Pallas kernels, backward(): pl.pallas_call(functools.partial(backward_kernel, count, first), out_shap...  40.5 us
    all_to_all x1, waiting for transfers between devices, fast_step(): lax.all_to_all(jnp.broadcast_to(residual.astype(bf16)[None], (owners, row...  22.1 us
    pallas_call x1, Pallas kernels, fast_step(): pl.pallas_call(pack_kernel, out_shape=[block] * owners, grid_spec=pltpu.P...  9.81 us
    pallas_call x1, Pallas kernels, fast_step(): pl.pallas_call(unpack_kernel, out_shape=jax.ShapeDtypeStruct(preacts.shap...  8.66 us
  transfers between devices with their start and end apart: 26, of which 15 were waited for; matrix products, arithmetic and copies ran while one was open for 2% of the time, Pallas kernels for 22%

profile of v1, /device:TPU:0, one launch (start us, length us, event | category | flops | bytes accessed | tf_op | source)
XLA Modules:
  0.0 278.1 jit_solution(1642920183437875862)
XLA Ops:
  4.3 9.8 %shard_map.167 = (bf16[1552,128]{1,0:T(8,128)(2,1)S(1)}, bf16[1552,128]{1,0:T(8,128)(2,1)S(1)}, bf16[1552,128]{1,0:T(8,128)(2,1)S(1)}, bf16[1552,128]{1,0:T(8,12...) custom-call(s32[6144]{0:T(1024)S(1)} %get-tuple-element.43.slot_sm, ...), custom_call_target="tpu_custom_call" | custom-call | tf_op jit(solution)/shard_map/pallas_call | solution.py:375
  14.9 3.0 %collective-permute-start.4 = (bf16[1552,128]{1,0:T(8,128)(2,1)S(1)}, bf16[1552,128]{1,0:T(8,128)(2,1)S(1)}, u32[]{:S(2)}, u32[]{:S(2)}) collective-permute-start(bf16[1552,128]{1,0:T(8,128)(2,1)S(1)} %get-tuple-element.26), channel_id=1, source_target_pairs={{0,2},{2,0},{4,6},{6,4},{8,10},{10,8},{12,14},{14,12},{1,3},{3,1},... | collective-permute-start | bytes 1191944 | tf_op jit(solution)/shard_map/ppermute | solution.py:370
  19.4 3.0 %collective-permute-start.2 = (bf16[1552,128]{1,0:T(8,128)(2,1)}, bf16[1552,128]{1,0:T(8,128)(2,1)S(1)}, u32[]{:S(2)}, u32[]{:S(2)}) collective-permute-start(bf16[1552,128]{1,0:T(8,128)(2,1)} %get-tuple-element.24), channel_id=1, source_target_pairs={{0,8},{2,10},{4,12},{6,14},{8,0},{10,2},{12,4},{14,6},{1,9},{3,11}... | collective-permute-start | bytes 1191944 | tf_op jit(solution)/shard_map/ppermute | solution.py:370
  23.7 6.5 %shard_map.168.refs_4_ = f32[384,2304]{1,0:T(8,128)S(1)} custom-call(s32[6]{0:T(128)S(1)} %copy-done.10, s32[1]{0:T(128)} %constant.138.clone.seq_sm, s32[1]{0:T(128)} %bitcast.me_sm, s32[1]{0:T(128)} %bitcast.1.half_sm, bf16[1552,128]{1,0:T(8,128)(2,1)S(1)} %get-tuple-element.29.refs_0_.all_refs_3_, bf16[12288,2304]{1,0:T(8,128)(2,1)} %bitcast.60), custom_call_target="tpu_custom_call" | custom-call | flops 2717908992 | bytes 7077888 | tf_op jit(solution)/shard_map/pallas_call | solution.py:417
  30.2 3.7 %collective-permute-start.1 = (bf16[1552,128]{1,0:T(8,128)(2,1)}, bf16[1552,128]{1,0:T(8,128)(2,1)S(1)}, u32[]{:S(2)}, u32[]{:S(2)}) collective-permute-start(bf16[1552,128]{1,0:T(8,128)(2,1)} %get-tuple-element.23), channel_id=1, source_target_pairs={{0,12},{2,14},{4,8},{6,10},{8,4},{10,6},{12,0},{14,2},{1,13},{3,15... | collective-permute-start | bytes 1191944 | tf_op jit(solution)/shard_map/ppermute | solution.py:370
  33.9 12.0 %collective-permute-done.5.refs_1_.all_refs_1_ = bf16[1552,128]{1,0:T(8,128)(2,1)S(1)} collective-permute-done((bf16[1552,128]{1,0:T(8,128)(2,1)S(1)}, bf16[1552,128]{1,0:T(8,128)(2,1)S(1)}, u32[]{:S(2)}, u32[]{:S(2)}) %collective-permute-start.5) | collective-permute-done | bytes 397344 | tf_op jit(solution)/shard_map/ppermute | solution.py:370
  46.8 5.3 %collective-permute-done.6.refs_2_.all_refs_0_ = bf16[1552,128]{1,0:T(8,128)(2,1)S(1)} collective-permute-done((bf16[1552,128]{1,0:T(8,128)(2,1)}, bf16[1552,128]{1,0:T(8,128)(2,1)S(1)}, u32[]{:S(2)}, u32[]{:S(2)}) %collective-permute-start.6) | collective-permute-done | bytes 397344 | tf_op jit(solution)/shard_map/ppermute | solution.py:370
  52.2 14.2 %shard_map.169.refs_3_ = f32[384,2304]{1,0:T(8,128)S(1)} custom-call(s32[6]{0:T(128)S(1)} %copy-done.10, s32[3]{0:T(128)S(1)} %copy-done.15, s32[1]{0:T(128)} %bitcast.me_sm, s32[1]{0:T(128)} %bitcast.1.half_sm, bf16[1552,128]{1,0:T(8,128)(2,1)S(1)} %collective-permute-done.4.refs_0_.all_refs_2_, ...), custom_call_target="tpu_custom_call" | custom-call | flops 8153726976 | bytes 21233664 | tf_op jit(solution)/shard_map/pallas_call | solution.py:417
  66.4 10.1 %collective-permute-done.3.refs_1_.all_refs_0_ = bf16[1552,128]{1,0:T(8,128)(2,1)S(1)} collective-permute-done((bf16[1552,128]{1,0:T(8,128)(2,1)}, bf16[1552,128]{1,0:T(8,128)(2,1)S(1)}, u32[]{:S(2)}, u32[]{:S(2)}) %collective-permute-start.3) | collective-permute-done | bytes 397344 | tf_op jit(solution)/shard_map/ppermute | solution.py:370
  76.5 10.3 %shard_map.170.refs_2_ = f32[384,2304]{1,0:T(8,128)S(1)} custom-call(s32[6]{0:T(128)S(1)} %copy-done.10, s32[2]{0:T(128)S(1)} %copy-done.12, s32[1]{0:T(128)} %bitcast.me_sm, s32[1]{0:T(128)} %bitcast.1.half_sm, bf16[1552,128]{1,0:T(8,128)(2,1)S(1)} %collective-permute-done.2.refs_0_.all_refs_0_, ...), custom_call_target="tpu_custom_call" | custom-call | flops 5435817984 | bytes 14155776 | tf_op jit(solution)/shard_map/pallas_call | solution.py:417
  86.9 6.5 %shard_map.171.refs_2_ = f32[384,2304]{1,0:T(8,128)S(1)} custom-call(s32[6]{0:T(128)S(1)} %copy-done.10, s32[1]{0:T(128)} %constant.141.clone.seq_sm, s32[1]{0:T(128)} %bitcast.me_sm, s32[1]{0:T(128)} %bitcast.1.half_sm, bf16[1552,128]{1,0:T(8,128)(2,1)S(1)} %collective-permute-done.1.refs_0_.all_refs_0_, bf16[12288,2304]{1,0:T(8,128)(2,1)} %bitcast.63, ...), custom_call_target="tpu_custom_call" | custom-call | flops 2717908992 | bytes 7077888 | tf_op jit(solution)/shard_map/pallas_call | solution.py:417
  93.4 7.5 %shard_map.172 = (f32[8,16,2304]{2,1,0:T(8,128)S(1)}, f32[8,8,2304]{2,1,0:T(8,128)S(1)}, f32[8,16,2304]{2,1,0:T(8,128)}, f32[8,8,2304]{2,1,0:T(8,128)S(1)}) custom-call(s32[6]{0:T(128)S(1)} %copy-done.10, s32[1]{0:T(128)} %constant.142.clone.seq_sm, s32[1]{0:T(128)} %bitcast.me_sm, s32[1]{0:T(128)} %bitcast.1.half_sm, ...), custom_call_target="tpu_custom_call" | custom-call | flops 2717908992 | bytes 7077888 | tf_op jit(solution)/shard_map/pallas_call | solution.py:417
  105.7 15.7 %collective-permute-done.13 = f32[4,8,2304]{2,1,0:T(8,128)} collective-permute-done((f32[4,8,2304]{2,1,0:T(8,128)}, f32[4,8,2304]{2,1,0:T(8,128)}, u32[]{:S(2)}, u32[]{:S(2)}) %collective-permute-start.13) | collective-permute-done | bytes 294944 | tf_op jit(solution)/shard_map/ppermute | solution.py:370
  122.4 1.7 add.179
  124.7 3.1 %collective-permute-start.9 = (f32[2,16,2304]{2,1,0:T(8,128)S(1)}, f32[2,16,2304]{2,1,0:T(8,128)S(1)}, u32[]{:S(2)}, u32[]{:S(2)}) collective-permute-start(f32[2,16,2304]{2,1,0:T(8,128)S(1)} %get-tuple-element.48), channel_id=1, source_target_pairs={{0,4},{2,6},{4,0},{6,2},{8,12},{10,14},{12,8},{14,10},{1,5},{3,7},... | collective-permute-start | bytes 884744 | tf_op jit(solution)/shard_map/ppermute | solution.py:370
  128.5 6.6 %collective-permute-done.10 = f32[2,16,2304]{2,1,0:T(8,128)S(1)} collective-permute-done((f32[2,16,2304]{2,1,0:T(8,128)S(1)}, f32[2,16,2304]{2,1,0:T(8,128)S(1)}, u32[]{:S(2)}, u32[]{:S(2)}) %collective-permute-start.10) | collective-permute-done | bytes 294944 | tf_op jit(solution)/shard_map/ppermute | solution.py:370
  135.1 4.6 %collective-permute-done.8 = f32[2,16,2304]{2,1,0:T(8,128)S(1)} collective-permute-done((f32[2,16,2304]{2,1,0:T(8,128)S(1)}, f32[2,16,2304]{2,1,0:T(8,128)S(1)}, u32[]{:S(2)}, u32[]{:S(2)}) %collective-permute-start.8) | collective-permute-done | bytes 294944 | tf_op jit(solution)/shard_map/ppermute | solution.py:370
  141.2 2.2 collective-permute-done.16
  143.5 4.6 %collective-permute-done.11 = f32[16,2304]{1,0:T(8,128)S(1)} collective-permute-done((f32[16,2304]{1,0:T(8,128)S(1)}, f32[16,2304]{1,0:T(8,128)S(1)}, u32[]{:S(2)}, u32[]{:S(2)}) %collective-permute-start.11) | collective-permute-done | bytes 147488 | tf_op jit(solution)/shard_map/ppermute | solution.py:370
  149.7 4.7 %all-to-all-start = ((bf16[8,24,2304]{2,1,0:T(8,128)(2,1)}), bf16[8,24,2304]{2,1,0:T(8,128)(2,1)S(1)}, u32[]{:S(2)}, u32[]{:S(2)}) async-start(bf16[8,24,2304]{2,1,0:T(8,128)(2,1)} %broadcast_in_dim.54), calls=%async_computation | async-start | bytes 1769472 | tf_op jit(solution)/shard_map/all_to_all | solution.py:467
  154.4 22.1 %all-to-all-done = bf16[8,24,2304]{2,1,0:T(8,128)(2,1)S(1)} async-done(((bf16[8,24,2304]{2,1,0:T(8,128)(2,1)}), bf16[8,24,2304]{2,1,0:T(8,128)(2,1)S(1)}, u32[]{:S(2)}, u32[]{:S(2)}) %all-to-all-start) | async-done | bytes 884768 | tf_op jit(solution)/shard_map/all_to_all | solution.py:467
  180.0 7.4 %shard_map.173 = (bf16[1536,128]{1,0:T(8,128)(2,1)S(1)}, bf16[384,2304]{1,0:T(8,128)(2,1)S(1)}) custom-call(s32[6]{0:T(128)S(1)} %copy-done.10, s32[1]{0:T(128)} %constant.143.clone.seq_sm, s32[1]{0:T(128)} %bitcast.me_sm, bf16[1552,128]{1,0:T(8,128)(2,1)S(1)} %collective-permute-done.2.refs_0_.all_refs_0_, bf16[12288,2304]{1,0:T(8,128)(2,1)} %bitcast.65, ...), custom_call_target="tpu_custom_call" | custom-call | flops 2717908992 | bytes 7077888 | tf_op jit(solution)/shard_map/pallas_call | solution.py:483
  187.4 9.8 %shard_map.176 = (bf16[1536,128]{1,0:T(8,128)(2,1)S(1)}, bf16[1536,128]{1,0:T(8,128)(2,1)S(1)}) custom-call(s32[6]{0:T(128)S(1)} %copy-done.10, s32[2]{0:T(128)S(1)} %copy-done.14, s32[1]{0:T(128)} %bitcast.me_sm, bf16[1552,128]{1,0:T(8,128)(2,1)S(1)} %collective-permute-done.1.refs_0_.all_refs_0_, ...), custom_call_target="tpu_custom_call" | custom-call | flops 5435817984 | bytes 14155776 | tf_op jit(solution)/shard_map/pallas_call | solution.py:483
  198.2 3.5 %collective-permute-start.24 = (bf16[1536,128]{1,0:T(8,128)(2,1)S(1)}, bf16[1536,128]{1,0:T(8,128)(2,1)S(1)}, u32[]{:S(2)}, u32[]{:S(2)}) collective-permute-start(bf16[1536,128]{1,0:T(8,128)(2,1)S(1)} %get-tuple-element.41), channel_id=1, source_target_pairs={{0,14},{2,12},{4,10},{6,8},{8,6},{10,4},{12,2},{14,0},{1,15},{3,13... | collective-permute-start | bytes 1179656 | tf_op jit(solution)/shard_map/ppermute | solution.py:370
  201.7 6.0 %shard_map.175 = bf16[1536,128]{1,0:T(8,128)(2,1)S(1)} custom-call(s32[6]{0:T(128)S(1)} %copy-done.10, s32[1]{0:T(128)} %constant.144.clone.seq_sm, s32[1]{0:T(128)} %bitcast.me_sm, bf16[1552,128]{1,0:T(8,128)(2,1)S(1)} %collective-permute-done.3.refs_1_.all_refs_0_, bf16[12288,2304]{1,0:T(8,128)(2,1)} %bitcast.67, ...), custom_call_target="tpu_custom_call" | custom-call | flops 2717908992 | bytes 7077888 | tf_op jit(solution)/shard_map/pallas_call | solution.py:483
  207.9 17.4 %shard_map.174 = (bf16[1536,128]{1,0:T(8,128)(2,1)S(1)}, bf16[1536,128]{1,0:T(8,128)(2,1)S(1)}, bf16[1536,128]{1,0:T(8,128)(2,1)S(1)}, bf16[1536,128]{1,0:T(8,128)(2,1)S(1)}) custom-call(s32[6]{0:T(128)S(1)} %copy-done.10, s32[4]{0:T(128)S(1)} %copy-done.11, s32[1]{0:T(128)} %bitcast.me_sm, bf16[1552,128]{1,0:T(8,128)(2,1)S(1)} %copy-done.5, ...), custom_call_target="tpu_custom_call" | custom-call | flops 10871635968 | bytes 28311552 | tf_op jit(solution)/shard_map/pallas_call | solution.py:483
  226.2 2.6 collective-permute-start.19
  228.8 5.1 %collective-permute-start.20 = (bf16[1536,128]{1,0:T(8,128)(2,1)S(1)}, bf16[1536,128]{1,0:T(8,128)(2,1)S(1)}, u32[]{:S(2)}, u32[]{:S(2)}) collective-permute-start(bf16[1536,128]{1,0:T(8,128)(2,1)S(1)} %get-tuple-element.38), channel_id=1, source_target_pairs={{0,6},{2,4},{4,2},{6,0},{8,14},{10,12},{12,10},{14,8},{1,7},{3,5},... | collective-permute-start | bytes 1179656 | tf_op jit(solution)/shard_map/ppermute | solution.py:370
  233.9 12.3 %collective-permute-start.21 = (bf16[1536,128]{1,0:T(8,128)(2,1)S(1)}, bf16[1536,128]{1,0:T(8,128)(2,1)S(1)}, u32[]{:S(2)}, u32[]{:S(2)}) collective-permute-start(bf16[1536,128]{1,0:T(8,128)(2,1)S(1)} %get-tuple-element.39), channel_id=1, source_target_pairs={{0,8},{2,10},{4,12},{6,14},{8,0},{10,2},{12,4},{14,6},{1,9},{3,11}... | collective-permute-start | bytes 1179656 | tf_op jit(solution)/shard_map/ppermute | solution.py:370
  246.9 14.2 %collective-permute-done.22.refs_5_ = bf16[1536,128]{1,0:T(8,128)(2,1)S(1)} collective-permute-done((bf16[1536,128]{1,0:T(8,128)(2,1)S(1)}, bf16[1536,128]{1,0:T(8,128)(2,1)S(1)}, u32[]{:S(2)}, u32[]{:S(2)}) %collective-permute-start.22) | collective-permute-done | bytes 393248 | tf_op jit(solution)/shard_map/ppermute | solution.py:370
  261.1 8.4 %collective-permute-done.21.refs_4_ = bf16[1536,128]{1,0:T(8,128)(2,1)S(1)} collective-permute-done((bf16[1536,128]{1,0:T(8,128)(2,1)S(1)}, bf16[1536,128]{1,0:T(8,128)(2,1)S(1)}, u32[]{:S(2)}, u32[]{:S(2)}) %collective-permute-start.21) | collective-permute-done | bytes 393248 | tf_op jit(solution)/shard_map/ppermute | solution.py:370
  269.5 8.7 %shard_map.177 = f32[3,1024,128]{2,1,0:T(8,128)} custom-call(s32[6144]{0:T(1024)S(1)} %copy-done.9, s32[6]{0:T(128)S(1)} %select_reduce_fusion.order_sm, bf16[1536,128]{1,0:T(8,128)(2,1)S(1)} %get-tuple-element.35.refs_0_, bf16[1536,128]{1,0:T(8,128)(2,1)S(1)} %collective-permute-done.18.refs_1_, bf16[1536,128]{1,0:T(8,128)(2,1)S(1)} %collective-permute-done.19.refs_2_, ...), custom_call_target="tpu_custom_call" | custom-call | tf_op jit(solution)/shard_map/pallas_call | solution.py:516
  (111 shorter events, 24.6 us)
Async XLA Ops:
  14.9 15.4 %collective-permute-start.4 = (bf16[1552,128]{1,0:T(8,128)(2,1)S(1)}, bf16[1552,128]{1,0:T(8,128)(2,1)S(1)}, u32[]{:S(2)}, u32[]{:S(2)}) collective-permute-start(bf16[1552,128]{1,0:T(8,128)(2,1)S(1)} %get-tuple-element.26), channel_id=1, source_target_pairs={{0,2},{2,0},{4,6},{6,4},{8,10},{10,8},{12,14},{14,12},{1,3},{3,1},... | collective-permute-start | bytes 1191944 | tf_op jit(solution)/shard_map/ppermute | solution.py:370
  17.8 28.1 %collective-permute-start.5 = (bf16[1552,128]{1,0:T(8,128)(2,1)S(1)}, bf16[1552,128]{1,0:T(8,128)(2,1)S(1)}, u32[]{:S(2)}, u32[]{:S(2)}) collective-permute-start(bf16[1552,128]{1,0:T(8,128)(2,1)S(1)} %get-tuple-element.27), channel_id=1, source_target_pairs={{0,4},{2,6},{4,0},{6,2},{8,12},{10,14},{12,8},{14,10},{1,5},{3,7},... | collective-permute-start | bytes 1191944 | tf_op jit(solution)/shard_map/ppermute | solution.py:370
  19.4 32.8 %collective-permute-start.6 = (bf16[1552,128]{1,0:T(8,128)(2,1)}, bf16[1552,128]{1,0:T(8,128)(2,1)S(1)}, u32[]{:S(2)}, u32[]{:S(2)}) collective-permute-start(bf16[1552,128]{1,0:T(8,128)(2,1)} %get-tuple-element.28), channel_id=1, source_target_pairs={{0,6},{2,4},{4,2},{6,0},{8,14},{10,12},{12,10},{14,8},{1,7},{3,5},... | collective-permute-start | bytes 1191944 | tf_op jit(solution)/shard_map/ppermute | solution.py:370
  19.4 47.0 %collective-permute-start.2 = (bf16[1552,128]{1,0:T(8,128)(2,1)}, bf16[1552,128]{1,0:T(8,128)(2,1)S(1)}, u32[]{:S(2)}, u32[]{:S(2)}) collective-permute-start(bf16[1552,128]{1,0:T(8,128)(2,1)} %get-tuple-element.24), channel_id=1, source_target_pairs={{0,8},{2,10},{4,12},{6,14},{8,0},{10,2},{12,4},{14,6},{1,9},{3,11}... | collective-permute-start | bytes 1191944 | tf_op jit(solution)/shard_map/ppermute | solution.py:370
  22.4 54.1 %collective-permute-start.3 = (bf16[1552,128]{1,0:T(8,128)(2,1)}, bf16[1552,128]{1,0:T(8,128)(2,1)S(1)}, u32[]{:S(2)}, u32[]{:S(2)}) collective-permute-start(bf16[1552,128]{1,0:T(8,128)(2,1)} %get-tuple-element.25), channel_id=1, source_target_pairs={{0,10},{2,8},{4,14},{6,12},{8,2},{10,0},{12,6},{14,4},{1,11},{3,9}... | collective-permute-start | bytes 1191944 | tf_op jit(solution)/shard_map/ppermute | solution.py:370
  23.7 22.2 %copy-start.17 = (bf16[1552,128]{1,0:T(8,128)(2,1)S(1)}, bf16[1552,128]{1,0:T(8,128)(2,1)}, u32[]{:S(2)}) copy-start(bf16[1552,128]{1,0:T(8,128)(2,1)} %copy-done.16) | copy-start | bytes 1191940
  23.7 28.5 %copy-start.15 = (s32[3]{0:T(128)S(1)}, s32[3]{0:T(128)}, u32[]{:S(2)}) copy-start(s32[3]{0:T(128)} %constant.139.clone.seq_sm) | copy-start | bytes 40
  30.2 56.6 %collective-permute-start.1 = (bf16[1552,128]{1,0:T(8,128)(2,1)}, bf16[1552,128]{1,0:T(8,128)(2,1)S(1)}, u32[]{:S(2)}, u32[]{:S(2)}) collective-permute-start(bf16[1552,128]{1,0:T(8,128)(2,1)} %get-tuple-element.23), channel_id=1, source_target_pairs={{0,12},{2,14},{4,8},{6,10},{8,4},{10,6},{12,0},{14,2},{1,13},{3,15... | collective-permute-start | bytes 1191944 | tf_op jit(solution)/shard_map/ppermute | solution.py:370
  45.9 30.6 %copy-start.12 = (s32[2]{0:T(128)S(1)}, s32[2]{0:T(128)}, u32[]{:S(2)}) copy-start(s32[2]{0:T(128)} %constant.140.clone.seq_sm) | copy-start | bytes 28
  45.9 47.5 %collective-permute-start = (bf16[1552,128]{1,0:T(8,128)(2,1)S(1)}, bf16[1552,128]{1,0:T(8,128)(2,1)S(1)}, u32[]{:S(2)}, u32[]{:S(2)}) collective-permute-start(bf16[1552,128]{1,0:T(8,128)(2,1)S(1)} %copy-done.17), channel_id=1, source_target_pairs={{0,14},{2,12},{4,10},{6,8},{8,6},{10,4},{12,2},{14,0},{1,15},{3,13... | collective-permute-start | bytes 1191944 | tf_op jit(solution)/shard_map/ppermute | solution.py:370
  102.0 2.0 collective-permute-start.12
  102.0 20.4 %collective-permute-start.7 = (f32[8,16,2304]{2,1,0:T(8,128)}, f32[8,16,2304]{2,1,0:T(8,128)}, u32[]{:S(2)}, u32[]{:S(2)}) collective-permute-start(f32[8,16,2304]{2,1,0:T(8,128)} %get-tuple-element.31), channel_id=1, source_target_pairs={{0,1},{1,0},{2,3},{3,2},{4,5},{5,4},{6,7},{7,6},{8,9},{9,8},{10,11... | collective-permute-start | bytes 3538952 | tf_op jit(solution)/shard_map/ppermute | solution.py:454
  104.8 16.6 %collective-permute-start.13 = (f32[4,8,2304]{2,1,0:T(8,128)}, f32[4,8,2304]{2,1,0:T(8,128)}, u32[]{:S(2)}, u32[]{:S(2)}) collective-permute-start(f32[4,8,2304]{2,1,0:T(8,128)} %slice.55), channel_id=1, source_target_pairs={{0,8},{2,10},{4,12},{6,14},{8,0},{10,2},{12,4},{14,6},{1,9},{3,11}... | collective-permute-start | bytes 884744 | tf_op jit(solution)/shard_map/ppermute | solution.py:370
  124.2 10.8 %collective-permute-start.10 = (f32[2,16,2304]{2,1,0:T(8,128)S(1)}, f32[2,16,2304]{2,1,0:T(8,128)S(1)}, u32[]{:S(2)}, u32[]{:S(2)}) collective-permute-start(f32[2,16,2304]{2,1,0:T(8,128)S(1)} %get-tuple-element.47), channel_id=1, source_target_pairs={{0,6},{2,4},{4,2},{6,0},{8,14},{10,12},{12,10},{14,8},{1,7},{3,5},... | collective-permute-start | bytes 884744 | tf_op jit(solution)/shard_map/ppermute | solution.py:370
  124.3 15.4 %collective-permute-start.8 = (f32[2,16,2304]{2,1,0:T(8,128)S(1)}, f32[2,16,2304]{2,1,0:T(8,128)S(1)}, u32[]{:S(2)}, u32[]{:S(2)}) collective-permute-start(f32[2,16,2304]{2,1,0:T(8,128)S(1)} %get-tuple-element.46), channel_id=1, source_target_pairs={{0,2},{2,0},{4,6},{6,4},{8,10},{10,8},{12,14},{14,12},{1,3},{3,1},... | collective-permute-start | bytes 884744 | tf_op jit(solution)/shard_map/ppermute | solution.py:370
  124.7 15.3 %collective-permute-start.9 = (f32[2,16,2304]{2,1,0:T(8,128)S(1)}, f32[2,16,2304]{2,1,0:T(8,128)S(1)}, u32[]{:S(2)}, u32[]{:S(2)}) collective-permute-start(f32[2,16,2304]{2,1,0:T(8,128)S(1)} %get-tuple-element.48), channel_id=1, source_target_pairs={{0,4},{2,6},{4,0},{6,2},{8,12},{10,14},{12,8},{14,10},{1,5},{3,7},... | collective-permute-start | bytes 884744 | tf_op jit(solution)/shard_map/ppermute | solution.py:370
  127.8 13.4 %collective-permute-start.14 = (f32[8,2304]{1,0:T(8,128)S(1)}, f32[8,2304]{1,0:T(8,128)S(1)}, u32[]{:S(2)}, u32[]{:S(2)}) collective-permute-start(f32[8,2304]{1,0:T(8,128)S(1)} %get-tuple-element.49), channel_id=1, source_target_pairs={{0,2},{2,0},{4,6},{6,4},{8,10},{10,8},{12,14},{14,12},{1,3},{3,1},... | collective-permute-start | bytes 221192 | tf_op jit(solution)/shard_map/ppermute | solution.py:370
  128.0 13.2 %collective-permute-start.15 = (f32[8,2304]{1,0:T(8,128)S(1)}, f32[8,2304]{1,0:T(8,128)S(1)}, u32[]{:S(2)}, u32[]{:S(2)}) collective-permute-start(f32[8,2304]{1,0:T(8,128)S(1)} %get-tuple-element.51), channel_id=1, source_target_pairs={{0,4},{2,6},{4,0},{6,2},{8,12},{10,14},{12,8},{14,10},{1,5},{3,7},... | collective-permute-start | bytes 221192 | tf_op jit(solution)/shard_map/ppermute | solution.py:370
  135.0 8.4 %collective-permute-start.16 = (f32[8,2304]{1,0:T(8,128)S(1)}, f32[8,2304]{1,0:T(8,128)S(1)}, u32[]{:S(2)}, u32[]{:S(2)}) collective-permute-start(f32[8,2304]{1,0:T(8,128)S(1)} %get-tuple-element.50), channel_id=1, source_target_pairs={{0,6},{2,4},{4,2},{6,0},{8,14},{10,12},{12,10},{14,8},{1,7},{3,5},... | collective-permute-start | bytes 221192 | tf_op jit(solution)/shard_map/ppermute | solution.py:370
  140.1 7.9 %collective-permute-start.11 = (f32[16,2304]{1,0:T(8,128)S(1)}, f32[16,2304]{1,0:T(8,128)S(1)}, u32[]{:S(2)}, u32[]{:S(2)}) collective-permute-start(f32[16,2304]{1,0:T(8,128)S(1)} %slice_bitcast_fusion.4), channel_id=1, source_target_pairs={{0,8},{2,10},{4,12},{6,14},{8,0},{10,2},{12,4},{14,6},{1,9},{3,11}... | collective-permute-start | bytes 442376 | tf_op jit(solution)/shard_map/ppermute | solution.py:370
  149.7 26.8 %all-to-all-start = ((bf16[8,24,2304]{2,1,0:T(8,128)(2,1)}), bf16[8,24,2304]{2,1,0:T(8,128)(2,1)S(1)}, u32[]{:S(2)}, u32[]{:S(2)}) async-start(bf16[8,24,2304]{2,1,0:T(8,128)(2,1)} %broadcast_in_dim.54), calls=%async_computation | async-start | bytes 1769472 | tf_op jit(solution)/shard_map/all_to_all | solution.py:467
  176.5 2.6 collective-permute-start.17
  197.2 31.6 %collective-permute-start.23 = (bf16[1536,128]{1,0:T(8,128)(2,1)S(1)}, bf16[1536,128]{1,0:T(8,128)(2,1)S(1)}, u32[]{:S(2)}, u32[]{:S(2)}) collective-permute-start(bf16[1536,128]{1,0:T(8,128)(2,1)S(1)} %get-tuple-element.40), channel_id=1, source_target_pairs={{0,12},{2,14},{4,8},{6,10},{8,4},{10,6},{12,0},{14,2},{1,13},{3,15... | collective-permute-start | bytes 1179656 | tf_op jit(solution)/shard_map/ppermute | solution.py:370
  198.2 35.7 %collective-permute-start.24 = (bf16[1536,128]{1,0:T(8,128)(2,1)S(1)}, bf16[1536,128]{1,0:T(8,128)(2,1)S(1)}, u32[]{:S(2)}, u32[]{:S(2)}) collective-permute-start(bf16[1536,128]{1,0:T(8,128)(2,1)S(1)} %get-tuple-element.41), channel_id=1, source_target_pairs={{0,14},{2,12},{4,10},{6,8},{8,6},{10,4},{12,2},{14,0},{1,15},{3,13... | collective-permute-start | bytes 1179656 | tf_op jit(solution)/shard_map/ppermute | solution.py:370
  207.7 38.5 %copy-start.19 = (bf16[3,16,1152]{2,1,0:T(8,128)(2,1)S(1)}, bf16[3,16,1152]{2,1,0:T(8,128)(2,1)}, u32[]{:S(2)}) copy-start(bf16[3,16,1152]{2,1,0:T(8,128)(2,1)} %param.17) | copy-start | bytes 331780
  207.7 61.7 %copy-start.1 = (bf16[3,1024,128]{2,1,0:T(8,128)(2,1)S(1)}, bf16[3,1024,128]{2,1,0:T(8,128)(2,1)}, u32[]{:S(2)}) copy-start(bf16[3,1024,128]{2,1,0:T(8,128)(2,1)} %refs_8_.1) | copy-start | bytes 2359300
  207.8 61.7 %copy-start.9 = (s32[6144]{0:T(1024)S(1)}, s32[6144]{0:T(1024)}, u32[]{:S(2)}) copy-start(s32[6144]{0:T(1024)} %copy-done.8) | copy-start | bytes 73732
  207.8 53.3 %collective-permute-start.22 = (bf16[1536,128]{1,0:T(8,128)(2,1)S(1)}, bf16[1536,128]{1,0:T(8,128)(2,1)S(1)}, u32[]{:S(2)}, u32[]{:S(2)}) collective-permute-start(bf16[1536,128]{1,0:T(8,128)(2,1)S(1)} %shard_map.175), channel_id=1, source_target_pairs={{0,10},{2,8},{4,14},{6,12},{8,2},{10,0},{12,6},{14,4},{1,11},{3,9}... | collective-permute-start | bytes 1179656 | tf_op jit(solution)/shard_map/ppermute | solution.py:370
  225.3 35.8 %collective-permute-start.18 = (bf16[1536,128]{1,0:T(8,128)(2,1)S(1)}, bf16[1536,128]{1,0:T(8,128)(2,1)S(1)}, u32[]{:S(2)}, u32[]{:S(2)}) collective-permute-start(bf16[1536,128]{1,0:T(8,128)(2,1)S(1)} %get-tuple-element.36), channel_id=1, source_target_pairs={{0,2},{2,0},{4,6},{6,4},{8,10},{10,8},{12,14},{14,12},{1,3},{3,1},... | collective-permute-start | bytes 1179656 | tf_op jit(solution)/shard_map/ppermute | solution.py:370
  226.2 34.9 %collective-permute-start.19 = (bf16[1536,128]{1,0:T(8,128)(2,1)S(1)}, bf16[1536,128]{1,0:T(8,128)(2,1)S(1)}, u32[]{:S(2)}, u32[]{:S(2)}) collective-permute-start(bf16[1536,128]{1,0:T(8,128)(2,1)S(1)} %get-tuple-element.37), channel_id=1, source_target_pairs={{0,4},{2,6},{4,0},{6,2},{8,12},{10,14},{12,8},{14,10},{1,5},{3,7},... | collective-permute-start | bytes 1179656 | tf_op jit(solution)/shard_map/ppermute | solution.py:370
  228.8 32.3 %collective-permute-start.20 = (bf16[1536,128]{1,0:T(8,128)(2,1)S(1)}, bf16[1536,128]{1,0:T(8,128)(2,1)S(1)}, u32[]{:S(2)}, u32[]{:S(2)}) collective-permute-start(bf16[1536,128]{1,0:T(8,128)(2,1)S(1)} %get-tuple-element.38), channel_id=1, source_target_pairs={{0,6},{2,4},{4,2},{6,0},{8,14},{10,12},{12,10},{14,8},{1,7},{3,5},... | collective-permute-start | bytes 1179656 | tf_op jit(solution)/shard_map/ppermute | solution.py:370
  233.9 35.5 %collective-permute-start.21 = (bf16[1536,128]{1,0:T(8,128)(2,1)S(1)}, bf16[1536,128]{1,0:T(8,128)(2,1)S(1)}, u32[]{:S(2)}, u32[]{:S(2)}) collective-permute-start(bf16[1536,128]{1,0:T(8,128)(2,1)S(1)} %get-tuple-element.39), channel_id=1, source_target_pairs={{0,8},{2,10},{4,12},{6,14},{8,0},{10,2},{12,4},{14,6},{1,9},{3,11}... | collective-permute-start | bytes 1179656 | tf_op jit(solution)/shard_map/ppermute | solution.py:370
  (15 other events, 102.2 us)

commit v2 on v1

--- a/solution.py
+++ b/solution.py
@@ -12,7 +12,7 @@
 UNROLL = 8
 NCOL = 768
 SPLIT = 2
-SEND_ORDER = (4, 1, 2, 3, 5, 6, 7)
+SEND_ORDER = (2, 1, 3, 4, 5, 6, 7)
 FORWARD_RUNS = ((0,), (1, 2, 3), (4, 5), (6,), (7,))
 BACKWARD_RUNS = ((4,), (5,), (6, 7), (3, 2, 1, 0))
 
@@ -161,10 +161,10 @@
     return target
 
 
-def forward_kernel(count, first, last, tgt_sm, seq_sm, me_sm, half_sm, *refs):
+def forward_kernel(count, first, last, ready, tgt_sm, seq_sm, me_sm, half_sm, *refs):
     recv_refs, w_ref, refs = refs[:count], refs[count], refs[count + 1 :]
     if not first:
-        before_ref, refs = refs[0], refs[1:]
+        before_ref, refs = refs[0], refs[1 + ready :]
     outs, (acc, lhs, goal, stage) = refs[:-4], refs[-4:]
     i = pl.program_id(0)
     depth, width = w_ref.shape
@@ -268,12 +268,19 @@
 
 
 def unpack_kernel(slot_sm, order_sm, *refs):
-    backs, (pre_ref, out_ref, rows) = refs[:-3], refs[-3:]
+    backs, (pre_ref, out_ref, rows, landed, sems) = refs[:-5], refs[-5:]
     layers, feats, _ = pre_ref.shape
     tiles = order_sm.shape[0]
     capacity = rows.shape[0] // len(backs)
-    for d, back_ref in enumerate(backs):
-        rows[d * capacity : (d + 1) * capacity, :] = back_ref[...].astype(jnp.float32)
+    copies = [
+        pltpu.make_async_copy(back_ref, landed.at[d], sems.at[d])
+        for d, back_ref in enumerate(backs)
+    ]
+    for copy in copies:
+        copy.start()
+    for d, copy in enumerate(copies):
+        copy.wait()
+        rows[d * capacity : (d + 1) * capacity, :] = landed[d].astype(jnp.float32)
     order = [order_sm[k] for k in range(tiles)]
 
     def step(i, carry):
@@ -352,7 +359,8 @@
     perm = (token_of[:, None] == lax.broadcasted_iota(i32, (1, tokens), 1)).astype(bf16)
     index = lax.broadcasted_iota(i32, (1, layers * tokens), 1)
     side = jnp.where(index // (owners * rows) == 0, my_half, 1 - my_half)
-    held = (index % (owners * rows)) // rows * 16 + side * 8 + index % 8
+    peer = lax.axis_index("tile") ^ (index % (owners * rows) // rows)
+    held = peer * 16 + side * 8 + index % 8
     held_layer = index % rows // 8
     wanted = jnp.tile(token_of, layers)[:, None]
     wanted_layer = lax.broadcasted_iota(i32, (layers * tokens, 1), 0) // tokens
@@ -404,7 +412,7 @@
     )
     whole = pl.BlockSpec(memory_space=pltpu.VMEM)
 
-    def forward(run, before, last):
+    def forward(number, run, before, last):
         first, count = before is None, len(run)
         if last:
             outs = [
@@ -414,14 +422,18 @@
         else:
             outs = [jax.ShapeDtypeStruct((layers * tokens, width), f32)]
         sums = [] if first else [before]
+        ready = [place, order] if number == 1 else []
         return pl.pallas_call(
-            functools.partial(forward_kernel, count, first, last),
+            functools.partial(forward_kernel, count, first, last, len(ready)),
             out_shape=outs,
             grid_spec=pltpu.PrefetchScalarGridSpec(
                 num_scalar_prefetch=4,
                 grid=(count * SPLIT,),
-                in_specs=[whole] * count + [weight_spec] + [whole] * len(sums),
-                out_specs=[whole] * len(outs),
+                in_specs=[whole] * count
+                + [weight_spec]
+                + [whole] * len(sums)
+                + [pl.BlockSpec(memory_space=pl.ANY)] * len(ready),
+                out_specs=[full(o.shape) for o in outs] if last else [whole],
                 scratch_shapes=[
                     pltpu.VMEM((layers * tokens, width), f32),
                     pltpu.VMEM((layers * tokens, capacity // SPLIT), bf16),
@@ -439,12 +451,13 @@
             *[received[d] for d in run],
             weights,
             *sums,
+            *ready,
         )
 
     value = None
     for number, run in enumerate(FORWARD_RUNS):
         last = number == len(FORWARD_RUNS) - 1
-        value = forward(run, value, last)
+        value = forward(number, run, value, last)
         if not last:
             value = value[0]
 
@@ -463,14 +476,16 @@
     for d in near:
         own_last = own_last + to_peer(d, last_sum[d])
     own_most = pair[0] + to_peer(mirror, pair[1])
-    residual = jnp.concatenate([own_most, own_last]) - targets.astype(f32).reshape(rows, width)
-    mine = lax.all_to_all(
-        jnp.broadcast_to(residual.astype(bf16)[None], (owners, rows, width)),
-        "tile",
-        split_axis=0,
-        concat_axis=0,
-        tiled=True,
-    ).reshape(owners * rows, width)
+    wanted = targets.astype(f32).reshape(rows, width)
+    own = [own_most - wanted[: rows - 8], own_last - wanted[rows - 8 :]]
+    spread = jnp.concatenate([o.astype(bf16) for o in own])
+    blocks = [spread] + [None] * (owners - 1)
+    blocks[mirror] = to_peer(mirror, spread)
+    for d in near:
+        blocks[d] = to_peer(d, spread)
+    for d in near:
+        blocks[mirror + d] = to_peer(d, blocks[mirror])
+    mine = jnp.concatenate(blocks)
     other = lax.ppermute(mine, "feat", swap)
 
     grad_block = jax.ShapeDtypeStruct((capacity, tokens), bf16)
@@ -519,13 +534,18 @@
         grid_spec=pltpu.PrefetchScalarGridSpec(
             num_scalar_prefetch=2,
             grid=(1,),
-            in_specs=[full(grad_block.shape)] * owners + [full(preacts.shape)],
+            in_specs=[pl.BlockSpec(memory_space=pltpu.HBM)] * owners + [full(preacts.shape)],
             out_specs=full(preacts.shape),
-            scratch_shapes=[pltpu.VMEM((slots, tokens), f32)],
+            scratch_shapes=[
+                pltpu.VMEM((slots, tokens), f32),
+                pltpu.VMEM((owners, capacity, tokens), bf16),
+                pltpu.SemaphoreType.DMA((owners,)),
+            ],
         ),
-        compiler_params=vmem(32),
+        compiler_params=vmem(60),
     )(slot, order, *returned, preacts)
-    return residual.reshape(targets.shape), feature_grad
+    residual = jnp.concatenate(own).reshape(targets.shape)
+    return residual, feature_grad
 
 
 def on_device(preacts, targets, decoder, owner_list, tile_source, tile_target, row_order):

time: 279 us -> 263 us (0.943)
  waiting for transfers between devices: 108 us -> 79.6 us
  starting transfers between devices: 50.2 us -> 61.9 us
  Pallas kernels: 104 us -> 108 us
    all_to_all x1 -> x0, waiting for transfers between devices: 22.1 us -> none  [fast_step(): lax.all_to_all(jnp.broadcast_to(residual.astype(bf16)[None], (owners, row...]
    ppermute x22 -> x29, starting transfers between devices: 45 us -> 61.3 us  [to_peer(): return lax.ppermute(block, 'tile', [(q, q ^ d) for q in range(owners)])]
    ppermute x22 -> x29, waiting for transfers between devices: 84.2 us -> 73.7 us  [to_peer(): return lax.ppermute(block, 'tile', [(q, q ^ d) for q in range(owners)])]
    all_to_all x1 -> x0, starting transfers between devices: 4.67 us -> none  [fast_step(): lax.all_to_all(jnp.broadcast_to(residual.astype(bf16)[None], (owners, row...]
  transfers between devices with their start and end apart: 26 -> 32, of which waited for: 15 -> 19; matrix products, arithmetic and copies ran while one was open for 2% -> 2% of each run, Pallas kernels for 22% -> 24%
where the time goes in v2:
time: 263 us; the launch traced here: 262 us
  Pallas kernels  108 us (41%)
  waiting for transfers between devices  79.6 us (30%)
  starting transfers between devices  61.9 us (24%)
  local copies, waits for them, and re-layouts  5.73 us (2%)
  other arithmetic  4.55 us (2%)
    ppermute x29, waiting for transfers between devices, to_peer(): return lax.ppermute(block, 'tile', [(q, q ^ d) for q in range(owners)])  73.7 us
    ppermute x29, starting transfers between devices, to_peer(): return lax.ppermute(block, 'tile', [(q, q ^ d) for q in range(owners)])  61.3 us
    pallas_call x5, Pallas kernels, forward(): pl.pallas_call(functools.partial(forward_kernel, count, first, last, len(...  45.3 us
    pallas_call x4, Pallas kernels, backward(): pl.pallas_call(functools.partial(backward_kernel, count, first), out_shap...  41.3 us
    pallas_call x1, Pallas kernels, fast_step(): pl.pallas_call(unpack_kernel, out_shape=jax.ShapeDtypeStruct(preacts.shap...  11.4 us
    pallas_call x1, Pallas kernels, fast_step(): pl.pallas_call(pack_kernel, out_shape=[block] * owners, grid_spec=pltpu.P...  9.93 us
  transfers between devices with their start and end apart: 32, of which 19 were waited for; matrix products, arithmetic and copies ran while one was open for 2% of the time, Pallas kernels for 24%

profile of v2, /device:TPU:0, one launch (start us, length us, event | category | flops | bytes accessed | tf_op | source)
XLA Modules:
  0.0 262.1 jit_solution(14958149640109028246)
XLA Ops:
  4.3 9.9 %shard_map.167 = (bf16[1552,128]{1,0:T(8,128)(2,1)S(1)}, bf16[1552,128]{1,0:T(8,128)(2,1)}, bf16[1552,128]{1,0:T(8,128)(2,1)}, bf16[1552,128]{1,0:T(8,128)(2,1)}...) custom-call(s32[6144]{0:T(1024)S(1)} %get-tuple-element.49.slot_sm, ...), custom_call_target="tpu_custom_call" | custom-call | tf_op jit(solution)/shard_map/pallas_call | solution.py:383
  14.9 3.0 %collective-permute-start.4 = (bf16[1552,128]{1,0:T(8,128)(2,1)}, bf16[1552,128]{1,0:T(8,128)(2,1)S(1)}, u32[]{:S(2)}, u32[]{:S(2)}) collective-permute-start(bf16[1552,128]{1,0:T(8,128)(2,1)} %get-tuple-element.26), channel_id=1, source_target_pairs={{0,2},{2,0},{4,6},{6,4},{8,10},{10,8},{12,14},{14,12},{1,3},{3,1},... | collective-permute-start | bytes 1191944 | tf_op jit(solution)/shard_map/ppermute | solution.py:378
  19.5 3.0 %collective-permute-start.2 = (bf16[1552,128]{1,0:T(8,128)(2,1)}, bf16[1552,128]{1,0:T(8,128)(2,1)S(1)}, u32[]{:S(2)}, u32[]{:S(2)}) collective-permute-start(bf16[1552,128]{1,0:T(8,128)(2,1)} %get-tuple-element.24), channel_id=1, source_target_pairs={{0,8},{2,10},{4,12},{6,14},{8,0},{10,2},{12,4},{14,6},{1,9},{3,11}... | collective-permute-start | bytes 1191944 | tf_op jit(solution)/shard_map/ppermute | solution.py:378
  24.3 6.5 %shard_map.168.refs_4_ = f32[384,2304]{1,0:T(8,128)S(1)} custom-call(s32[6]{0:T(128)S(1)} %copy-done.8, s32[1]{0:T(128)} %constant.138.clone.seq_sm, s32[1]{0:T(128)} %bitcast.me_sm, s32[1]{0:T(128)} %bitcast.1.half_sm, bf16[1552,128]{1,0:T(8,128)(2,1)S(1)} %get-tuple-element.29.refs_0_.all_refs_3_, bf16[12288,2304]{1,0:T(8,128)(2,1)} %bitcast.65), custom_call_target="tpu_custom_call" | custom-call | flops 2717908992 | bytes 7077888 | tf_op jit(solution)/shard_map/pallas_call | solution.py:426
  30.9 3.7 %collective-permute-start.1 = (bf16[1552,128]{1,0:T(8,128)(2,1)S(1)}, bf16[1552,128]{1,0:T(8,128)(2,1)S(1)}, u32[]{:S(2)}, u32[]{:S(2)}) collective-permute-start(bf16[1552,128]{1,0:T(8,128)(2,1)S(1)} %copy-done.16), channel_id=1, source_target_pairs={{0,12},{2,14},{4,8},{6,10},{8,4},{10,6},{12,0},{14,2},{1,13},{3,15... | collective-permute-start | bytes 1191944 | tf_op jit(solution)/shard_map/ppermute | solution.py:378
  34.6 11.7 %collective-permute-done.5.refs_1_.all_refs_1_ = bf16[1552,128]{1,0:T(8,128)(2,1)S(1)} collective-permute-done((bf16[1552,128]{1,0:T(8,128)(2,1)}, bf16[1552,128]{1,0:T(8,128)(2,1)S(1)}, u32[]{:S(2)}, u32[]{:S(2)}) %collective-permute-start.5) | collective-permute-done | bytes 397344 | tf_op jit(solution)/shard_map/ppermute | solution.py:378
  47.3 5.2 %collective-permute-done.6.refs_2_.all_refs_0_ = bf16[1552,128]{1,0:T(8,128)(2,1)S(1)} collective-permute-done((bf16[1552,128]{1,0:T(8,128)(2,1)}, bf16[1552,128]{1,0:T(8,128)(2,1)S(1)}, u32[]{:S(2)}, u32[]{:S(2)}) %collective-permute-start.6) | collective-permute-done | bytes 397344 | tf_op jit(solution)/shard_map/ppermute | solution.py:378
  52.6 14.2 %shard_map.169.refs_3_ = f32[384,2304]{1,0:T(8,128)S(1)} custom-call(s32[6]{0:T(128)S(1)} %copy-done.8, s32[3]{0:T(128)S(1)} %copy-done.14, s32[1]{0:T(128)} %bitcast.me_sm, s32[1]{0:T(128)} %bitcast.1.half_sm, bf16[1552,128]{1,0:T(8,128)(2,1)S(1)} %collective-permute-done.4.refs_0_.all_refs_2_, ...), custom_call_target="tpu_custom_call" | custom-call | flops 8153726976 | bytes 21233664 | tf_op jit(solution)/shard_map/pallas_call | solution.py:426
  66.7 9.8 %collective-permute-done.3.refs_1_.all_refs_0_ = bf16[1552,128]{1,0:T(8,128)(2,1)S(1)} collective-permute-done((bf16[1552,128]{1,0:T(8,128)(2,1)}, bf16[1552,128]{1,0:T(8,128)(2,1)S(1)}, u32[]{:S(2)}, u32[]{:S(2)}) %collective-permute-start.3) | collective-permute-done | bytes 397344 | tf_op jit(solution)/shard_map/ppermute | solution.py:378
  76.6 10.3 %shard_map.170.refs_2_ = f32[384,2304]{1,0:T(8,128)S(1)} custom-call(s32[6]{0:T(128)S(1)} %copy-done.8, s32[2]{0:T(128)S(1)} %copy-done.11, s32[1]{0:T(128)} %bitcast.me_sm, s32[1]{0:T(128)} %bitcast.1.half_sm, bf16[1552,128]{1,0:T(8,128)(2,1)S(1)} %collective-permute-done.2.refs_0_.all_refs_0_, ...), custom_call_target="tpu_custom_call" | custom-call | flops 5435817984 | bytes 14155776 | tf_op jit(solution)/shard_map/pallas_call | solution.py:426
  86.9 6.5 %shard_map.171.refs_2_ = f32[384,2304]{1,0:T(8,128)S(1)} custom-call(s32[6]{0:T(128)S(1)} %copy-done.8, s32[1]{0:T(128)} %constant.141.clone.seq_sm, s32[1]{0:T(128)} %bitcast.me_sm, s32[1]{0:T(128)} %bitcast.1.half_sm, bf16[1552,128]{1,0:T(8,128)(2,1)S(1)} %collective-permute-done.1.refs_0_.all_refs_0_, bf16[12288,2304]{1,0:T(8,128)(2,1)} %bitcast.68, ...), custom_call_target="tpu_custom_call" | custom-call | flops 2717908992 | bytes 7077888 | tf_op jit(solution)/shard_map/pallas_call | solution.py:426
  93.5 7.7 %shard_map.172 = (f32[8,16,2304]{2,1,0:T(8,128)S(1)}, f32[8,8,2304]{2,1,0:T(8,128)S(1)}, f32[8,16,2304]{2,1,0:T(8,128)}, f32[8,8,2304]{2,1,0:T(8,128)}) custom-call(s32[6]{0:T(128)S(1)} %copy-done.8, s32[1]{0:T(128)} %constant.142.clone.seq_sm, s32[1]{0:T(128)} %bitcast.me_sm, s32[1]{0:T(128)} %bitcast.1.half_sm, ...), custom_call_target="tpu_custom_call" | custom-call | flops 2717908992 | bytes 7077888 | tf_op jit(solution)/shard_map/pallas_call | solution.py:426
  103.8 3.4 %collective-permute-done.12 = f32[8,8,2304]{2,1,0:T(8,128)} collective-permute-done((f32[8,8,2304]{2,1,0:T(8,128)}, f32[8,8,2304]{2,1,0:T(8,128)}, u32[]{:S(2)}, u32[]{:S(2)}) %collective-permute-start.12) | collective-permute-done | bytes 589856 | tf_op jit(solution)/shard_map/ppermute | solution.py:466
  110.9 3.3 %collective-permute-start.10 = (f32[2,16,2304]{2,1,0:T(8,128)S(1)}, f32[2,16,2304]{2,1,0:T(8,128)S(1)}, u32[]{:S(2)}, u32[]{:S(2)}) collective-permute-start(f32[2,16,2304]{2,1,0:T(8,128)S(1)} %get-tuple-element.54), channel_id=1, source_target_pairs={{0,6},{2,4},{4,2},{6,0},{8,14},{10,12},{12,10},{14,8},{1,7},{3,5},... | collective-permute-start | bytes 884744 | tf_op jit(solution)/shard_map/ppermute | solution.py:378
  115.7 9.2 %collective-permute-done.13 = f32[4,8,2304]{2,1,0:T(8,128)S(1)} collective-permute-done((f32[4,8,2304]{2,1,0:T(8,128)S(1)}, f32[4,8,2304]{2,1,0:T(8,128)S(1)}, u32[]{:S(2)}, u32[]{:S(2)}) %collective-permute-start.13) | collective-permute-done | bytes 294944 | tf_op jit(solution)/shard_map/ppermute | solution.py:378
  127.6 5.3 %collective-permute-done.9 = f32[2,16,2304]{2,1,0:T(8,128)S(1)} collective-permute-done((f32[2,16,2304]{2,1,0:T(8,128)S(1)}, f32[2,16,2304]{2,1,0:T(8,128)S(1)}, u32[]{:S(2)}, u32[]{:S(2)}) %collective-permute-start.9) | collective-permute-done | bytes 294944 | tf_op jit(solution)/shard_map/ppermute | solution.py:378
  135.2 2.5 collective-permute-start.15
  137.7 4.5 %collective-permute-done.11 = f32[16,2304]{1,0:T(8,128)S(1)} collective-permute-done((f32[16,2304]{1,0:T(8,128)S(1)}, f32[16,2304]{1,0:T(8,128)S(1)}, u32[]{:S(2)}, u32[]{:S(2)}) %collective-permute-start.11) | collective-permute-done | bytes 147488 | tf_op jit(solution)/shard_map/ppermute | solution.py:378
  145.3 2.4 collective-permute-start.18
  147.6 2.4 collective-permute-done.20
  151.3 3.1 %collective-permute-start.23 = (bf16[24,2304]{1,0:T(8,128)(2,1)S(1)}, bf16[24,2304]{1,0:T(8,128)(2,1)S(1)}, u32[]{:S(2)}, u32[]{:S(2)}) collective-permute-start(bf16[24,2304]{1,0:T(8,128)(2,1)S(1)} %collective-permute-done.20), channel_id=1, source_target_pairs={{0,6},{2,4},{4,2},{6,0},{8,14},{10,12},{12,10},{14,8},{1,7},{3,5},... | collective-permute-start | bytes 331784 | tf_op jit(solution)/shard_map/ppermute | solution.py:378
  158.7 2.4 collective-permute-done.24.all_refs_3_
  161.1 7.1 %shard_map.173 = (bf16[1536,128]{1,0:T(8,128)(2,1)S(1)}, bf16[384,2304]{1,0:T(8,128)(2,1)S(1)}) custom-call(s32[6]{0:T(128)S(1)} %copy-done.8, s32[1]{0:T(128)} %constant.143.clone.seq_sm, s32[1]{0:T(128)} %bitcast.me_sm, bf16[1552,128]{1,0:T(8,128)(2,1)S(1)} %collective-permute-done.2.refs_0_.all_refs_0_, bf16[12288,2304]{1,0:T(8,128)(2,1)} %bitcast.70, ...), custom_call_target="tpu_custom_call" | custom-call | flops 2717908992 | bytes 7077888 | tf_op jit(solution)/shard_map/pallas_call | solution.py:498
  168.2 9.8 %shard_map.176 = (bf16[1536,128]{1,0:T(8,128)(2,1)S(1)}, bf16[1536,128]{1,0:T(8,128)(2,1)S(1)}) custom-call(s32[6]{0:T(128)S(1)} %copy-done.8, s32[2]{0:T(128)S(1)} %copy-done.13, s32[1]{0:T(128)} %bitcast.me_sm, bf16[1552,128]{1,0:T(8,128)(2,1)S(1)} %collective-permute-done.1.refs_0_.all_refs_0_, bf16[1552,128]{1,0:T(8,128)(2,1)S(1)} %copy-done.2, ...), custom_call_target="tpu_custom_call" | custom-call | flops 5435817984 | bytes 14155776 | tf_op jit(solution)/shard_map/pallas_call | solution.py:498
  178.1 2.3 collective-permute-start.30
  182.5 6.0 %shard_map.175 = bf16[1536,128]{1,0:T(8,128)(2,1)S(1)} custom-call(s32[6]{0:T(128)S(1)} %copy-done.8, s32[1]{0:T(128)} %constant.144.clone.seq_sm, s32[1]{0:T(128)} %bitcast.me_sm, bf16[1552,128]{1,0:T(8,128)(2,1)S(1)} %collective-permute-done.3.refs_1_.all_refs_0_, bf16[12288,2304]{1,0:T(8,128)(2,1)} %bitcast.72, ...), custom_call_target="tpu_custom_call" | custom-call | flops 2717908992 | bytes 7077888 | tf_op jit(solution)/shard_map/pallas_call | solution.py:498
  188.6 18.3 %shard_map.174 = (bf16[1536,128]{1,0:T(8,128)(2,1)}, bf16[1536,128]{1,0:T(8,128)(2,1)}, bf16[1536,128]{1,0:T(8,128)(2,1)S(1)}, bf16[1536,128]{1,0:T(8,128)(2,1)S(1)}) custom-call(s32[6]{0:T(128)S(1)} %copy-done.8, s32[4]{0:T(128)S(1)} %copy-done.10, s32[1]{0:T(128)} %bitcast.me_sm, bf16[1552,128]{1,0:T(8,128)(2,1)S(1)} %collective-permute-done.6.refs_2_.all_refs_0_, ...), custom_call_target="tpu_custom_call" | custom-call | flops 10871635968 | bytes 28311552 | tf_op jit(solution)/shard_map/pallas_call | solution.py:498
  211.1 5.8 %collective-permute-start.27 = (bf16[1536,128]{1,0:T(8,128)(2,1)}, bf16[1536,128]{1,0:T(8,128)(2,1)S(1)}, u32[]{:S(2)}, u32[]{:S(2)}) collective-permute-start(bf16[1536,128]{1,0:T(8,128)(2,1)} %get-tuple-element.38), channel_id=1, source_target_pairs={{0,6},{2,4},{4,2},{6,0},{8,14},{10,12},{12,10},{14,8},{1,7},{3,5},... | collective-permute-start | bytes 1179656 | tf_op jit(solution)/shard_map/ppermute | solution.py:378
  216.9 14.3 %collective-permute-start.28 = (bf16[1536,128]{1,0:T(8,128)(2,1)S(1)}, bf16[1536,128]{1,0:T(8,128)(2,1)S(1)}, u32[]{:S(2)}, u32[]{:S(2)}) collective-permute-start(bf16[1536,128]{1,0:T(8,128)(2,1)S(1)} %get-tuple-element.39), channel_id=1, source_target_pairs={{0,8},{2,10},{4,12},{6,14},{8,0},{10,2},{12,4},{14,6},{1,9},{3,11}... | collective-permute-start | bytes 1179656 | tf_op jit(solution)/shard_map/ppermute | solution.py:378
  231.9 12.5 %collective-permute-done.29.refs_5_ = bf16[1536,128]{1,0:T(8,128)(2,1)} collective-permute-done((bf16[1536,128]{1,0:T(8,128)(2,1)S(1)}, bf16[1536,128]{1,0:T(8,128)(2,1)}, u32[]{:S(2)}, u32[]{:S(2)}) %collective-permute-start.29) | collective-permute-done | bytes 393248 | tf_op jit(solution)/shard_map/ppermute | solution.py:378
  244.4 5.3 %collective-permute-done.28.refs_4_ = bf16[1536,128]{1,0:T(8,128)(2,1)S(1)} collective-permute-done((bf16[1536,128]{1,0:T(8,128)(2,1)S(1)}, bf16[1536,128]{1,0:T(8,128)(2,1)S(1)}, u32[]{:S(2)}, u32[]{:S(2)}) %collective-permute-start.28) | collective-permute-done | bytes 393248 | tf_op jit(solution)/shard_map/ppermute | solution.py:378
  250.5 11.4 %shard_map.177 = f32[3,1024,128]{2,1,0:T(8,128)} custom-call(s32[6144]{0:T(1024)} %copy-done.6, s32[6]{0:T(128)} %copy-done.9, bf16[1536,128]{1,0:T(8,128)(2,1)} %copy-done.7, bf16[1536,128]{1,0:T(8,128)(2,1)} %copy-done.20, bf16[1536,128]{1,0:T(8,128)(2,1)} %copy-done.21, bf16[1536,128]{1,0:T(8,128)(2,1)} %copy-done.22, bf16[1536,128]{1,0:T(8,128)(2,1)} %copy-done.23, ...), custom_call_target="tpu_custom_call" | custom-call | tf_op jit(solution)/shard_map/pallas_call | solution.py:531
  (140 shorter events, 37.8 us)
Async XLA Ops:
  14.9 15.9 %collective-permute-start.4 = (bf16[1552,128]{1,0:T(8,128)(2,1)}, bf16[1552,128]{1,0:T(8,128)(2,1)S(1)}, u32[]{:S(2)}, u32[]{:S(2)}) collective-permute-start(bf16[1552,128]{1,0:T(8,128)(2,1)} %get-tuple-element.26), channel_id=1, source_target_pairs={{0,2},{2,0},{4,6},{6,4},{8,10},{10,8},{12,14},{14,12},{1,3},{3,1},... | collective-permute-start | bytes 1191944 | tf_op jit(solution)/shard_map/ppermute | solution.py:378
  17.9 28.4 %collective-permute-start.5 = (bf16[1552,128]{1,0:T(8,128)(2,1)}, bf16[1552,128]{1,0:T(8,128)(2,1)S(1)}, u32[]{:S(2)}, u32[]{:S(2)}) collective-permute-start(bf16[1552,128]{1,0:T(8,128)(2,1)} %get-tuple-element.27), channel_id=1, source_target_pairs={{0,4},{2,6},{4,0},{6,2},{8,12},{10,14},{12,8},{14,10},{1,5},{3,7},... | collective-permute-start | bytes 1191944 | tf_op jit(solution)/shard_map/ppermute | solution.py:378
  19.5 33.1 %collective-permute-start.6 = (bf16[1552,128]{1,0:T(8,128)(2,1)}, bf16[1552,128]{1,0:T(8,128)(2,1)S(1)}, u32[]{:S(2)}, u32[]{:S(2)}) collective-permute-start(bf16[1552,128]{1,0:T(8,128)(2,1)} %get-tuple-element.28), channel_id=1, source_target_pairs={{0,6},{2,4},{4,2},{6,0},{8,14},{10,12},{12,10},{14,8},{1,7},{3,5},... | collective-permute-start | bytes 1191944 | tf_op jit(solution)/shard_map/ppermute | solution.py:378
  19.5 47.3 %collective-permute-start.2 = (bf16[1552,128]{1,0:T(8,128)(2,1)}, bf16[1552,128]{1,0:T(8,128)(2,1)S(1)}, u32[]{:S(2)}, u32[]{:S(2)}) collective-permute-start(bf16[1552,128]{1,0:T(8,128)(2,1)} %get-tuple-element.24), channel_id=1, source_target_pairs={{0,8},{2,10},{4,12},{6,14},{8,0},{10,2},{12,4},{14,6},{1,9},{3,11}... | collective-permute-start | bytes 1191944 | tf_op jit(solution)/shard_map/ppermute | solution.py:378
  22.5 54.1 %collective-permute-start.3 = (bf16[1552,128]{1,0:T(8,128)(2,1)}, bf16[1552,128]{1,0:T(8,128)(2,1)S(1)}, u32[]{:S(2)}, u32[]{:S(2)}) collective-permute-start(bf16[1552,128]{1,0:T(8,128)(2,1)} %get-tuple-element.25), channel_id=1, source_target_pairs={{0,10},{2,8},{4,14},{6,12},{8,2},{10,0},{12,6},{14,4},{1,11},{3,9}... | collective-permute-start | bytes 1191944 | tf_op jit(solution)/shard_map/ppermute | solution.py:378
  30.9 56.1 %collective-permute-start.1 = (bf16[1552,128]{1,0:T(8,128)(2,1)S(1)}, bf16[1552,128]{1,0:T(8,128)(2,1)S(1)}, u32[]{:S(2)}, u32[]{:S(2)}) collective-permute-start(bf16[1552,128]{1,0:T(8,128)(2,1)S(1)} %copy-done.16), channel_id=1, source_target_pairs={{0,12},{2,14},{4,8},{6,10},{8,4},{10,6},{12,0},{14,2},{1,13},{3,15... | collective-permute-start | bytes 1191944 | tf_op jit(solution)/shard_map/ppermute | solution.py:378
  46.3 47.2 %collective-permute-start = (bf16[1552,128]{1,0:T(8,128)(2,1)S(1)}, bf16[1552,128]{1,0:T(8,128)(2,1)S(1)}, u32[]{:S(2)}, u32[]{:S(2)}) collective-permute-start(bf16[1552,128]{1,0:T(8,128)(2,1)S(1)} %get-tuple-element.22), channel_id=1, source_target_pairs={{0,14},{2,12},{4,10},{6,8},{8,6},{10,4},{12,2},{14,0},{1,15},{3,13... | collective-permute-start | bytes 1191944 | tf_op jit(solution)/shard_map/ppermute | solution.py:378
  103.1 6.3 %collective-permute-start.7 = (f32[8,16,2304]{2,1,0:T(8,128)}, f32[8,16,2304]{2,1,0:T(8,128)}, u32[]{:S(2)}, u32[]{:S(2)}) collective-permute-start(f32[8,16,2304]{2,1,0:T(8,128)} %get-tuple-element.31), channel_id=1, source_target_pairs={{0,1},{1,0},{2,3},{3,2},{4,5},{5,4},{6,7},{7,6},{8,9},{9,8},{10,11... | collective-permute-start | bytes 3538952 | tf_op jit(solution)/shard_map/ppermute | solution.py:467
  103.1 4.0 %collective-permute-start.12 = (f32[8,8,2304]{2,1,0:T(8,128)}, f32[8,8,2304]{2,1,0:T(8,128)}, u32[]{:S(2)}, u32[]{:S(2)}) collective-permute-start(f32[8,8,2304]{2,1,0:T(8,128)} %get-tuple-element.33), channel_id=1, source_target_pairs={{0,1},{1,0},{2,3},{3,2},{4,5},{5,4},{6,7},{7,6},{8,9},{9,8},{10,11... | collective-permute-start | bytes 1769480 | tf_op jit(solution)/shard_map/ppermute | solution.py:466
  108.5 16.4 %collective-permute-start.13 = (f32[4,8,2304]{2,1,0:T(8,128)S(1)}, f32[4,8,2304]{2,1,0:T(8,128)S(1)}, u32[]{:S(2)}, u32[]{:S(2)}) collective-permute-start(f32[4,8,2304]{2,1,0:T(8,128)S(1)} %slice.72), channel_id=1, source_target_pairs={{0,8},{2,10},{4,12},{6,14},{8,0},{10,2},{12,4},{14,6},{1,9},{3,11}... | collective-permute-start | bytes 884744 | tf_op jit(solution)/shard_map/ppermute | solution.py:378
  110.9 16.2 %collective-permute-start.10 = (f32[2,16,2304]{2,1,0:T(8,128)S(1)}, f32[2,16,2304]{2,1,0:T(8,128)S(1)}, u32[]{:S(2)}, u32[]{:S(2)}) collective-permute-start(f32[2,16,2304]{2,1,0:T(8,128)S(1)} %get-tuple-element.54), channel_id=1, source_target_pairs={{0,6},{2,4},{4,2},{6,0},{8,14},{10,12},{12,10},{14,8},{1,7},{3,5},... | collective-permute-start | bytes 884744 | tf_op jit(solution)/shard_map/ppermute | solution.py:378
  114.3 13.3 %collective-permute-start.8 = (f32[2,16,2304]{2,1,0:T(8,128)S(1)}, f32[2,16,2304]{2,1,0:T(8,128)S(1)}, u32[]{:S(2)}, u32[]{:S(2)}) collective-permute-start(f32[2,16,2304]{2,1,0:T(8,128)S(1)} %get-tuple-element.52), channel_id=1, source_target_pairs={{0,2},{2,0},{4,6},{6,4},{8,10},{10,8},{12,14},{14,12},{1,3},{3,1},... | collective-permute-start | bytes 884744 | tf_op jit(solution)/shard_map/ppermute | solution.py:378
  115.7 17.2 %collective-permute-start.9 = (f32[2,16,2304]{2,1,0:T(8,128)S(1)}, f32[2,16,2304]{2,1,0:T(8,128)S(1)}, u32[]{:S(2)}, u32[]{:S(2)}) collective-permute-start(f32[2,16,2304]{2,1,0:T(8,128)S(1)} %get-tuple-element.53), channel_id=1, source_target_pairs={{0,4},{2,6},{4,0},{6,2},{8,12},{10,14},{12,8},{14,10},{1,5},{3,7},... | collective-permute-start | bytes 884744 | tf_op jit(solution)/shard_map/ppermute | solution.py:378
  133.0 9.1 %collective-permute-start.11 = (f32[16,2304]{1,0:T(8,128)S(1)}, f32[16,2304]{1,0:T(8,128)S(1)}, u32[]{:S(2)}, u32[]{:S(2)}) collective-permute-start(f32[16,2304]{1,0:T(8,128)S(1)} %slice_bitcast_fusion.4), channel_id=1, source_target_pairs={{0,8},{2,10},{4,12},{6,14},{8,0},{10,2},{12,4},{14,6},{1,9},{3,11}... | collective-permute-start | bytes 442376 | tf_op jit(solution)/shard_map/ppermute | solution.py:378
  133.6 8.5 %collective-permute-start.14 = (f32[8,2304]{1,0:T(8,128)S(1)}, f32[8,2304]{1,0:T(8,128)S(1)}, u32[]{:S(2)}, u32[]{:S(2)}) collective-permute-start(f32[8,2304]{1,0:T(8,128)S(1)} %get-tuple-element.55), channel_id=1, source_target_pairs={{0,2},{2,0},{4,6},{6,4},{8,10},{10,8},{12,14},{14,12},{1,3},{3,1},... | collective-permute-start | bytes 221192 | tf_op jit(solution)/shard_map/ppermute | solution.py:378
  135.2 7.7 %collective-permute-start.15 = (f32[8,2304]{1,0:T(8,128)S(1)}, f32[8,2304]{1,0:T(8,128)S(1)}, u32[]{:S(2)}, u32[]{:S(2)}) collective-permute-start(f32[8,2304]{1,0:T(8,128)S(1)} %get-tuple-element.57), channel_id=1, source_target_pairs={{0,4},{2,6},{4,0},{6,2},{8,12},{10,14},{12,8},{14,10},{1,5},{3,7},... | collective-permute-start | bytes 221192 | tf_op jit(solution)/shard_map/ppermute | solution.py:378
  137.6 5.6 %collective-permute-start.16 = (f32[8,2304]{1,0:T(8,128)S(1)}, f32[8,2304]{1,0:T(8,128)S(1)}, u32[]{:S(2)}, u32[]{:S(2)}) collective-permute-start(f32[8,2304]{1,0:T(8,128)S(1)} %get-tuple-element.56), channel_id=1, source_target_pairs={{0,6},{2,4},{4,2},{6,0},{8,14},{10,12},{12,10},{14,8},{1,7},{3,5},... | collective-permute-start | bytes 221192 | tf_op jit(solution)/shard_map/ppermute | solution.py:378
  143.3 6.7 %collective-permute-start.20 = (bf16[24,2304]{1,0:T(8,128)(2,1)S(1)}, bf16[24,2304]{1,0:T(8,128)(2,1)S(1)}, u32[]{:S(2)}, u32[]{:S(2)}) collective-permute-start(bf16[24,2304]{1,0:T(8,128)(2,1)S(1)} %pad_maximum_fusion.1), channel_id=1, source_target_pairs={{0,8},{2,10},{4,12},{6,14},{8,0},{10,2},{12,4},{14,6},{1,9},{3,11}... | collective-permute-start | bytes 331784 | tf_op jit(solution)/shard_map/ppermute | solution.py:378
  143.7 7.6 %collective-permute-start.17 = (bf16[24,2304]{1,0:T(8,128)(2,1)S(1)}, bf16[24,2304]{1,0:T(8,128)(2,1)S(1)}, u32[]{:S(2)}, u32[]{:S(2)}) collective-permute-start(bf16[24,2304]{1,0:T(8,128)(2,1)S(1)} %pad_maximum_fusion.1), channel_id=1, source_target_pairs={{0,2},{2,0},{4,6},{6,4},{8,10},{10,8},{12,14},{14,12},{1,3},{3,1},... | collective-permute-start | bytes 331784 | tf_op jit(solution)/shard_map/ppermute | solution.py:378
  145.3 9.1 %collective-permute-start.18 = (bf16[24,2304]{1,0:T(8,128)(2,1)S(1)}, bf16[24,2304]{1,0:T(8,128)(2,1)S(1)}, u32[]{:S(2)}, u32[]{:S(2)}) collective-permute-start(bf16[24,2304]{1,0:T(8,128)(2,1)S(1)} %pad_maximum_fusion.1), channel_id=1, source_target_pairs={{0,4},{2,6},{4,0},{6,2},{8,12},{10,14},{12,8},{14,10},{1,5},{3,7},... | collective-permute-start | bytes 331784 | tf_op jit(solution)/shard_map/ppermute | solution.py:378
  147.6 7.1 %collective-permute-start.19 = (bf16[24,2304]{1,0:T(8,128)(2,1)S(1)}, bf16[24,2304]{1,0:T(8,128)(2,1)S(1)}, u32[]{:S(2)}, u32[]{:S(2)}) collective-permute-start(bf16[24,2304]{1,0:T(8,128)(2,1)S(1)} %pad_maximum_fusion.1), channel_id=1, source_target_pairs={{0,6},{2,4},{4,2},{6,0},{8,14},{10,12},{12,10},{14,8},{1,7},{3,5},... | collective-permute-start | bytes 331784 | tf_op jit(solution)/shard_map/ppermute | solution.py:378
  150.0 6.5 %collective-permute-start.21 = (bf16[24,2304]{1,0:T(8,128)(2,1)S(1)}, bf16[24,2304]{1,0:T(8,128)(2,1)S(1)}, u32[]{:S(2)}, u32[]{:S(2)}) collective-permute-start(bf16[24,2304]{1,0:T(8,128)(2,1)S(1)} %collective-permute-done.20), channel_id=1, source_target_pairs={{0,2},{2,0},{4,6},{6,4},{8,10},{10,8},{12,14},{14,12},{1,3},{3,1},... | collective-permute-start | bytes 331784 | tf_op jit(solution)/shard_map/ppermute | solution.py:378
  151.3 5.7 %collective-permute-start.22 = (bf16[24,2304]{1,0:T(8,128)(2,1)S(1)}, bf16[24,2304]{1,0:T(8,128)(2,1)S(1)}, u32[]{:S(2)}, u32[]{:S(2)}) collective-permute-start(bf16[24,2304]{1,0:T(8,128)(2,1)S(1)} %collective-permute-done.20), channel_id=1, source_target_pairs={{0,4},{2,6},{4,0},{6,2},{8,12},{10,14},{12,8},{14,10},{1,5},{3,7},... | collective-permute-start | bytes 331784 | tf_op jit(solution)/shard_map/ppermute | solution.py:378
  151.3 7.3 %collective-permute-start.23 = (bf16[24,2304]{1,0:T(8,128)(2,1)S(1)}, bf16[24,2304]{1,0:T(8,128)(2,1)S(1)}, u32[]{:S(2)}, u32[]{:S(2)}) collective-permute-start(bf16[24,2304]{1,0:T(8,128)(2,1)S(1)} %collective-permute-done.20), channel_id=1, source_target_pairs={{0,6},{2,4},{4,2},{6,0},{8,14},{10,12},{12,10},{14,8},{1,7},{3,5},... | collective-permute-start | bytes 331784 | tf_op jit(solution)/shard_map/ppermute | solution.py:378
  158.6 2.5 collective-permute-start.24
  178.1 33.0 %collective-permute-start.30 = (bf16[1536,128]{1,0:T(8,128)(2,1)S(1)}, bf16[1536,128]{1,0:T(8,128)(2,1)S(1)}, u32[]{:S(2)}, u32[]{:S(2)}) collective-permute-start(bf16[1536,128]{1,0:T(8,128)(2,1)S(1)} %get-tuple-element.40), channel_id=1, source_target_pairs={{0,12},{2,14},{4,8},{6,10},{8,4},{10,6},{12,0},{14,2},{1,13},{3,15... | collective-permute-start | bytes 1179656 | tf_op jit(solution)/shard_map/ppermute | solution.py:378
  180.4 36.5 %collective-permute-start.31 = (bf16[1536,128]{1,0:T(8,128)(2,1)S(1)}, bf16[1536,128]{1,0:T(8,128)(2,1)S(1)}, u32[]{:S(2)}, u32[]{:S(2)}) collective-permute-start(bf16[1536,128]{1,0:T(8,128)(2,1)S(1)} %get-tuple-element.41), channel_id=1, source_target_pairs={{0,14},{2,12},{4,10},{6,8},{8,6},{10,4},{12,2},{14,0},{1,15},{3,13... | collective-permute-start | bytes 1179656 | tf_op jit(solution)/shard_map/ppermute | solution.py:378
  188.5 55.9 %collective-permute-start.29 = (bf16[1536,128]{1,0:T(8,128)(2,1)S(1)}, bf16[1536,128]{1,0:T(8,128)(2,1)}, u32[]{:S(2)}, u32[]{:S(2)}) collective-permute-start(bf16[1536,128]{1,0:T(8,128)(2,1)S(1)} %shard_map.175), channel_id=1, source_target_pairs={{0,10},{2,8},{4,14},{6,12},{8,2},{10,0},{12,6},{14,4},{1,11},{3,9}... | collective-permute-start | bytes 1179656 | tf_op jit(solution)/shard_map/ppermute | solution.py:378
  206.9 37.4 %collective-permute-start.25 = (bf16[1536,128]{1,0:T(8,128)(2,1)S(1)}, bf16[1536,128]{1,0:T(8,128)(2,1)S(1)}, u32[]{:S(2)}, u32[]{:S(2)}) collective-permute-start(bf16[1536,128]{1,0:T(8,128)(2,1)S(1)} %get-tuple-element.36), channel_id=1, source_target_pairs={{0,2},{2,0},{4,6},{6,4},{8,10},{10,8},{12,14},{14,12},{1,3},{3,1},... | collective-permute-start | bytes 1179656 | tf_op jit(solution)/shard_map/ppermute | solution.py:378
  208.9 35.5 %collective-permute-start.26 = (bf16[1536,128]{1,0:T(8,128)(2,1)}, bf16[1536,128]{1,0:T(8,128)(2,1)S(1)}, u32[]{:S(2)}, u32[]{:S(2)}) collective-permute-start(bf16[1536,128]{1,0:T(8,128)(2,1)} %get-tuple-element.37), channel_id=1, source_target_pairs={{0,4},{2,6},{4,0},{6,2},{8,12},{10,14},{12,8},{14,10},{1,5},{3,7},... | collective-permute-start | bytes 1179656 | tf_op jit(solution)/shard_map/ppermute | solution.py:378
  211.1 33.3 %collective-permute-start.27 = (bf16[1536,128]{1,0:T(8,128)(2,1)}, bf16[1536,128]{1,0:T(8,128)(2,1)S(1)}, u32[]{:S(2)}, u32[]{:S(2)}) collective-permute-start(bf16[1536,128]{1,0:T(8,128)(2,1)} %get-tuple-element.38), channel_id=1, source_target_pairs={{0,6},{2,4},{4,2},{6,0},{8,14},{10,12},{12,10},{14,8},{1,7},{3,5},... | collective-permute-start | bytes 1179656 | tf_op jit(solution)/shard_map/ppermute | solution.py:378
  216.9 32.9 %collective-permute-start.28 = (bf16[1536,128]{1,0:T(8,128)(2,1)S(1)}, bf16[1536,128]{1,0:T(8,128)(2,1)S(1)}, u32[]{:S(2)}, u32[]{:S(2)}) collective-permute-start(bf16[1536,128]{1,0:T(8,128)(2,1)S(1)} %get-tuple-element.39), channel_id=1, source_target_pairs={{0,8},{2,10},{4,12},{6,14},{8,0},{10,2},{12,4},{14,6},{1,9},{3,11}... | collective-permute-start | bytes 1179656 | tf_op jit(solution)/shard_map/ppermute | solution.py:378
  (25 other events, 266.6 us)

commit v3 on v2

--- a/solution.py
+++ b/solution.py
@@ -9,7 +9,7 @@
 
 
 META = 16
-UNROLL = 8
+UNROLL = 16
 NCOL = 768
 SPLIT = 2
 SEND_ORDER = (2, 1, 3, 4, 5, 6, 7)
@@ -140,11 +140,12 @@
     bases = [src_sm[k] * feats for k in range(tiles)]
 
     def step(i, carry):
+        unit = i * (UNROLL * tiles)
+        at = [base + i * UNROLL for base in bases]
         for j in range(UNROLL):
-            f = i * UNROLL + j
             for k in range(tiles):
-                slot = slot_sm[f * tiles + k]
-                packed[pl.ds(slot, 1), :] = nat[pl.ds(bases[k] + f, 1), :]
+                slot = slot_sm[unit + (j * tiles + k)]
+                packed[pl.ds(slot, 1), :] = nat[pl.ds(at[k] + j, 1), :]
         return carry
 
     lax.fori_loop(0, feats // UNROLL, step, 0)
@@ -284,13 +285,14 @@
     order = [order_sm[k] for k in range(tiles)]
 
     def step(i, carry):
+        at = [i * (UNROLL * tiles) + o for o in order]
         for j in range(UNROLL):
             f = i * UNROLL + j
             k = 0
             for s in range(layers):
                 total = None
                 for _ in range(layers - s):
-                    row = rows[pl.ds(slot_sm[f * tiles + order[k]], 1), :]
+                    row = rows[pl.ds(slot_sm[at[k] + j * tiles], 1), :]
                     total = row if total is None else total + row
                     k += 1
                 out_ref[s, pl.ds(f, 1), :] = total

time: 263 us -> 261 us (level)
  Pallas kernels: 108 us -> 105 us
where the time goes in v3:
time: 261 us; the launch traced here: 259 us
  Pallas kernels  105 us (40%)
  waiting for transfers between devices  79.5 us (30%)
  starting transfers between devices  61.9 us (24%)
  local copies, waits for them, and re-layouts  5.73 us (2%)
  other arithmetic  4.55 us (2%)
    ppermute x29, waiting for transfers between devices, to_peer(): return lax.ppermute(block, 'tile', [(q, q ^ d) for q in range(owners)])  73.7 us
    ppermute x29, starting transfers between devices, to_peer(): return lax.ppermute(block, 'tile', [(q, q ^ d) for q in range(owners)])  61.3 us
    pallas_call x5, Pallas kernels, forward(): pl.pallas_call(functools.partial(forward_kernel, count, first, last, len(...  45.3 us
    pallas_call x4, Pallas kernels, backward(): pl.pallas_call(functools.partial(backward_kernel, count, first), out_shap...  41.3 us
    pallas_call x1, Pallas kernels, fast_step(): pl.pallas_call(unpack_kernel, out_shape=jax.ShapeDtypeStruct(preacts.shap...  10.6 us
    pallas_call x1, Pallas kernels, fast_step(): pl.pallas_call(pack_kernel, out_shape=[block] * owners, grid_spec=pltpu.P...  8.04 us
  transfers between devices with their start and end apart: 32, of which 19 were waited for; matrix products, arithmetic and copies ran while one was open for 2% of the time, Pallas kernels for 24%

profile of v3, /device:TPU:0, one launch (start us, length us, event | category | flops | bytes accessed | tf_op | source)
XLA Modules:
  0.0 259.4 jit_solution(6642225885895137646)
XLA Ops:
  4.3 8.0 %shard_map.167 = (bf16[1552,128]{1,0:T(8,128)(2,1)S(1)}, bf16[1552,128]{1,0:T(8,128)(2,1)}, bf16[1552,128]{1,0:T(8,128)(2,1)}, bf16[1552,128]{1,0:T(8,128)(2,1)}...) custom-call(s32[6144]{0:T(1024)S(1)} %get-tuple-element.49.slot_sm, ...), custom_call_target="tpu_custom_call" | custom-call | tf_op jit(solution)/shard_map/pallas_call | solution.py:385
  13.0 3.0 %collective-permute-start.4 = (bf16[1552,128]{1,0:T(8,128)(2,1)}, bf16[1552,128]{1,0:T(8,128)(2,1)S(1)}, u32[]{:S(2)}, u32[]{:S(2)}) collective-permute-start(bf16[1552,128]{1,0:T(8,128)(2,1)} %get-tuple-element.26), channel_id=1, source_target_pairs={{0,2},{2,0},{4,6},{6,4},{8,10},{10,8},{12,14},{14,12},{1,3},{3,1},... | collective-permute-start | bytes 1191944 | tf_op jit(solution)/shard_map/ppermute | solution.py:380
  17.6 3.0 %collective-permute-start.2 = (bf16[1552,128]{1,0:T(8,128)(2,1)}, bf16[1552,128]{1,0:T(8,128)(2,1)S(1)}, u32[]{:S(2)}, u32[]{:S(2)}) collective-permute-start(bf16[1552,128]{1,0:T(8,128)(2,1)} %get-tuple-element.24), channel_id=1, source_target_pairs={{0,8},{2,10},{4,12},{6,14},{8,0},{10,2},{12,4},{14,6},{1,9},{3,11}... | collective-permute-start | bytes 1191944 | tf_op jit(solution)/shard_map/ppermute | solution.py:380
  22.4 6.5 %shard_map.168.refs_4_ = f32[384,2304]{1,0:T(8,128)S(1)} custom-call(s32[6]{0:T(128)S(1)} %copy-done.8, s32[1]{0:T(128)} %constant.138.clone.seq_sm, s32[1]{0:T(128)} %bitcast.me_sm, s32[1]{0:T(128)} %bitcast.1.half_sm, bf16[1552,128]{1,0:T(8,128)(2,1)S(1)} %get-tuple-element.29.refs_0_.all_refs_3_, bf16[12288,2304]{1,0:T(8,128)(2,1)} %bitcast.65), custom_call_target="tpu_custom_call" | custom-call | flops 2717908992 | bytes 7077888 | tf_op jit(solution)/shard_map/pallas_call | solution.py:428
  29.0 3.7 %collective-permute-start.1 = (bf16[1552,128]{1,0:T(8,128)(2,1)S(1)}, bf16[1552,128]{1,0:T(8,128)(2,1)S(1)}, u32[]{:S(2)}, u32[]{:S(2)}) collective-permute-start(bf16[1552,128]{1,0:T(8,128)(2,1)S(1)} %copy-done.16), channel_id=1, source_target_pairs={{0,12},{2,14},{4,8},{6,10},{8,4},{10,6},{12,0},{14,2},{1,13},{3,15... | collective-permute-start | bytes 1191944 | tf_op jit(solution)/shard_map/ppermute | solution.py:380
  32.7 11.7 %collective-permute-done.5.refs_1_.all_refs_1_ = bf16[1552,128]{1,0:T(8,128)(2,1)S(1)} collective-permute-done((bf16[1552,128]{1,0:T(8,128)(2,1)}, bf16[1552,128]{1,0:T(8,128)(2,1)S(1)}, u32[]{:S(2)}, u32[]{:S(2)}) %collective-permute-start.5) | collective-permute-done | bytes 397344 | tf_op jit(solution)/shard_map/ppermute | solution.py:380
  45.4 5.2 %collective-permute-done.6.refs_2_.all_refs_0_ = bf16[1552,128]{1,0:T(8,128)(2,1)S(1)} collective-permute-done((bf16[1552,128]{1,0:T(8,128)(2,1)}, bf16[1552,128]{1,0:T(8,128)(2,1)S(1)}, u32[]{:S(2)}, u32[]{:S(2)}) %collective-permute-start.6) | collective-permute-done | bytes 397344 | tf_op jit(solution)/shard_map/ppermute | solution.py:380
  50.7 14.2 %shard_map.169.refs_3_ = f32[384,2304]{1,0:T(8,128)S(1)} custom-call(s32[6]{0:T(128)S(1)} %copy-done.8, s32[3]{0:T(128)S(1)} %copy-done.14, s32[1]{0:T(128)} %bitcast.me_sm, s32[1]{0:T(128)} %bitcast.1.half_sm, bf16[1552,128]{1,0:T(8,128)(2,1)S(1)} %collective-permute-done.4.refs_0_.all_refs_2_, ...), custom_call_target="tpu_custom_call" | custom-call | flops 8153726976 | bytes 21233664 | tf_op jit(solution)/shard_map/pallas_call | solution.py:428
  64.9 9.8 %collective-permute-done.3.refs_1_.all_refs_0_ = bf16[1552,128]{1,0:T(8,128)(2,1)S(1)} collective-permute-done((bf16[1552,128]{1,0:T(8,128)(2,1)}, bf16[1552,128]{1,0:T(8,128)(2,1)S(1)}, u32[]{:S(2)}, u32[]{:S(2)}) %collective-permute-start.3) | collective-permute-done | bytes 397344 | tf_op jit(solution)/shard_map/ppermute | solution.py:380
  74.7 10.3 %shard_map.170.refs_2_ = f32[384,2304]{1,0:T(8,128)S(1)} custom-call(s32[6]{0:T(128)S(1)} %copy-done.8, s32[2]{0:T(128)S(1)} %copy-done.11, s32[1]{0:T(128)} %bitcast.me_sm, s32[1]{0:T(128)} %bitcast.1.half_sm, bf16[1552,128]{1,0:T(8,128)(2,1)S(1)} %collective-permute-done.2.refs_0_.all_refs_0_, ...), custom_call_target="tpu_custom_call" | custom-call | flops 5435817984 | bytes 14155776 | tf_op jit(solution)/shard_map/pallas_call | solution.py:428
  85.1 6.5 %shard_map.171.refs_2_ = f32[384,2304]{1,0:T(8,128)S(1)} custom-call(s32[6]{0:T(128)S(1)} %copy-done.8, s32[1]{0:T(128)} %constant.141.clone.seq_sm, s32[1]{0:T(128)} %bitcast.me_sm, s32[1]{0:T(128)} %bitcast.1.half_sm, bf16[1552,128]{1,0:T(8,128)(2,1)S(1)} %collective-permute-done.1.refs_0_.all_refs_0_, bf16[12288,2304]{1,0:T(8,128)(2,1)} %bitcast.68, ...), custom_call_target="tpu_custom_call" | custom-call | flops 2717908992 | bytes 7077888 | tf_op jit(solution)/shard_map/pallas_call | solution.py:428
  91.6 7.7 %shard_map.172 = (f32[8,16,2304]{2,1,0:T(8,128)S(1)}, f32[8,8,2304]{2,1,0:T(8,128)S(1)}, f32[8,16,2304]{2,1,0:T(8,128)}, f32[8,8,2304]{2,1,0:T(8,128)}) custom-call(s32[6]{0:T(128)S(1)} %copy-done.8, s32[1]{0:T(128)} %constant.142.clone.seq_sm, s32[1]{0:T(128)} %bitcast.me_sm, s32[1]{0:T(128)} %bitcast.1.half_sm, ...), custom_call_target="tpu_custom_call" | custom-call | flops 2717908992 | bytes 7077888 | tf_op jit(solution)/shard_map/pallas_call | solution.py:428
  101.9 3.4 %collective-permute-done.12 = f32[8,8,2304]{2,1,0:T(8,128)} collective-permute-done((f32[8,8,2304]{2,1,0:T(8,128)}, f32[8,8,2304]{2,1,0:T(8,128)}, u32[]{:S(2)}, u32[]{:S(2)}) %collective-permute-start.12) | collective-permute-done | bytes 589856 | tf_op jit(solution)/shard_map/ppermute | solution.py:468
  109.0 3.3 %collective-permute-start.10 = (f32[2,16,2304]{2,1,0:T(8,128)S(1)}, f32[2,16,2304]{2,1,0:T(8,128)S(1)}, u32[]{:S(2)}, u32[]{:S(2)}) collective-permute-start(f32[2,16,2304]{2,1,0:T(8,128)S(1)} %get-tuple-element.54), channel_id=1, source_target_pairs={{0,6},{2,4},{4,2},{6,0},{8,14},{10,12},{12,10},{14,8},{1,7},{3,5},... | collective-permute-start | bytes 884744 | tf_op jit(solution)/shard_map/ppermute | solution.py:380
  113.9 9.2 %collective-permute-done.13 = f32[4,8,2304]{2,1,0:T(8,128)S(1)} collective-permute-done((f32[4,8,2304]{2,1,0:T(8,128)S(1)}, f32[4,8,2304]{2,1,0:T(8,128)S(1)}, u32[]{:S(2)}, u32[]{:S(2)}) %collective-permute-start.13) | collective-permute-done | bytes 294944 | tf_op jit(solution)/shard_map/ppermute | solution.py:380
  125.7 5.3 %collective-permute-done.9 = f32[2,16,2304]{2,1,0:T(8,128)S(1)} collective-permute-done((f32[2,16,2304]{2,1,0:T(8,128)S(1)}, f32[2,16,2304]{2,1,0:T(8,128)S(1)}, u32[]{:S(2)}, u32[]{:S(2)}) %collective-permute-start.9) | collective-permute-done | bytes 294944 | tf_op jit(solution)/shard_map/ppermute | solution.py:380
  133.3 2.5 collective-permute-start.15
  135.8 4.5 %collective-permute-done.11 = f32[16,2304]{1,0:T(8,128)S(1)} collective-permute-done((f32[16,2304]{1,0:T(8,128)S(1)}, f32[16,2304]{1,0:T(8,128)S(1)}, u32[]{:S(2)}, u32[]{:S(2)}) %collective-permute-start.11) | collective-permute-done | bytes 147488 | tf_op jit(solution)/shard_map/ppermute | solution.py:380
  143.4 2.3 collective-permute-start.18
  145.7 2.4 collective-permute-done.20
  149.4 3.1 %collective-permute-start.23 = (bf16[24,2304]{1,0:T(8,128)(2,1)S(1)}, bf16[24,2304]{1,0:T(8,128)(2,1)S(1)}, u32[]{:S(2)}, u32[]{:S(2)}) collective-permute-start(bf16[24,2304]{1,0:T(8,128)(2,1)S(1)} %collective-permute-done.20), channel_id=1, source_target_pairs={{0,6},{2,4},{4,2},{6,0},{8,14},{10,12},{12,10},{14,8},{1,7},{3,5},... | collective-permute-start | bytes 331784 | tf_op jit(solution)/shard_map/ppermute | solution.py:380
  156.8 2.4 collective-permute-done.24.all_refs_3_
  159.2 7.1 %shard_map.173 = (bf16[1536,128]{1,0:T(8,128)(2,1)S(1)}, bf16[384,2304]{1,0:T(8,128)(2,1)S(1)}) custom-call(s32[6]{0:T(128)S(1)} %copy-done.8, s32[1]{0:T(128)} %constant.143.clone.seq_sm, s32[1]{0:T(128)} %bitcast.me_sm, bf16[1552,128]{1,0:T(8,128)(2,1)S(1)} %collective-permute-done.2.refs_0_.all_refs_0_, bf16[12288,2304]{1,0:T(8,128)(2,1)} %bitcast.70, ...), custom_call_target="tpu_custom_call" | custom-call | flops 2717908992 | bytes 7077888 | tf_op jit(solution)/shard_map/pallas_call | solution.py:500
  166.4 9.8 %shard_map.176 = (bf16[1536,128]{1,0:T(8,128)(2,1)S(1)}, bf16[1536,128]{1,0:T(8,128)(2,1)S(1)}) custom-call(s32[6]{0:T(128)S(1)} %copy-done.8, s32[2]{0:T(128)S(1)} %copy-done.13, s32[1]{0:T(128)} %bitcast.me_sm, bf16[1552,128]{1,0:T(8,128)(2,1)S(1)} %collective-permute-done.1.refs_0_.all_refs_0_, bf16[1552,128]{1,0:T(8,128)(2,1)S(1)} %copy-done.2, ...), custom_call_target="tpu_custom_call" | custom-call | flops 5435817984 | bytes 14155776 | tf_op jit(solution)/shard_map/pallas_call | solution.py:500
  176.2 2.3 collective-permute-start.30
  180.6 6.0 %shard_map.175 = bf16[1536,128]{1,0:T(8,128)(2,1)S(1)} custom-call(s32[6]{0:T(128)S(1)} %copy-done.8, s32[1]{0:T(128)} %constant.144.clone.seq_sm, s32[1]{0:T(128)} %bitcast.me_sm, bf16[1552,128]{1,0:T(8,128)(2,1)S(1)} %collective-permute-done.3.refs_1_.all_refs_0_, bf16[12288,2304]{1,0:T(8,128)(2,1)} %bitcast.72, ...), custom_call_target="tpu_custom_call" | custom-call | flops 2717908992 | bytes 7077888 | tf_op jit(solution)/shard_map/pallas_call | solution.py:500
  186.7 18.3 %shard_map.174 = (bf16[1536,128]{1,0:T(8,128)(2,1)}, bf16[1536,128]{1,0:T(8,128)(2,1)}, bf16[1536,128]{1,0:T(8,128)(2,1)S(1)}, bf16[1536,128]{1,0:T(8,128)(2,1)S(1)}) custom-call(s32[6]{0:T(128)S(1)} %copy-done.8, s32[4]{0:T(128)S(1)} %copy-done.10, s32[1]{0:T(128)} %bitcast.me_sm, bf16[1552,128]{1,0:T(8,128)(2,1)S(1)} %collective-permute-done.6.refs_2_.all_refs_0_, ...), custom_call_target="tpu_custom_call" | custom-call | flops 10871635968 | bytes 28311552 | tf_op jit(solution)/shard_map/pallas_call | solution.py:500
  209.2 5.7 %collective-permute-start.27 = (bf16[1536,128]{1,0:T(8,128)(2,1)}, bf16[1536,128]{1,0:T(8,128)(2,1)S(1)}, u32[]{:S(2)}, u32[]{:S(2)}) collective-permute-start(bf16[1536,128]{1,0:T(8,128)(2,1)} %get-tuple-element.38), channel_id=1, source_target_pairs={{0,6},{2,4},{4,2},{6,0},{8,14},{10,12},{12,10},{14,8},{1,7},{3,5},... | collective-permute-start | bytes 1179656 | tf_op jit(solution)/shard_map/ppermute | solution.py:380
  215.0 14.3 %collective-permute-start.28 = (bf16[1536,128]{1,0:T(8,128)(2,1)S(1)}, bf16[1536,128]{1,0:T(8,128)(2,1)S(1)}, u32[]{:S(2)}, u32[]{:S(2)}) collective-permute-start(bf16[1536,128]{1,0:T(8,128)(2,1)S(1)} %get-tuple-element.39), channel_id=1, source_target_pairs={{0,8},{2,10},{4,12},{6,14},{8,0},{10,2},{12,4},{14,6},{1,9},{3,11}... | collective-permute-start | bytes 1179656 | tf_op jit(solution)/shard_map/ppermute | solution.py:380
  230.1 12.5 %collective-permute-done.29.refs_5_ = bf16[1536,128]{1,0:T(8,128)(2,1)} collective-permute-done((bf16[1536,128]{1,0:T(8,128)(2,1)S(1)}, bf16[1536,128]{1,0:T(8,128)(2,1)}, u32[]{:S(2)}, u32[]{:S(2)}) %collective-permute-start.29) | collective-permute-done | bytes 393248 | tf_op jit(solution)/shard_map/ppermute | solution.py:380
  242.6 5.3 %collective-permute-done.28.refs_4_ = bf16[1536,128]{1,0:T(8,128)(2,1)S(1)} collective-permute-done((bf16[1536,128]{1,0:T(8,128)(2,1)S(1)}, bf16[1536,128]{1,0:T(8,128)(2,1)S(1)}, u32[]{:S(2)}, u32[]{:S(2)}) %collective-permute-start.28) | collective-permute-done | bytes 393248 | tf_op jit(solution)/shard_map/ppermute | solution.py:380
  248.6 10.6 %shard_map.177 = f32[3,1024,128]{2,1,0:T(8,128)} custom-call(s32[6144]{0:T(1024)} %copy-done.6, s32[6]{0:T(128)} %copy-done.9, bf16[1536,128]{1,0:T(8,128)(2,1)} %copy-done.7, bf16[1536,128]{1,0:T(8,128)(2,1)} %copy-done.20, bf16[1536,128]{1,0:T(8,128)(2,1)} %copy-done.21, bf16[1536,128]{1,0:T(8,128)(2,1)} %copy-done.22, bf16[1536,128]{1,0:T(8,128)(2,1)} %copy-done.23, ...), custom_call_target="tpu_custom_call" | custom-call | tf_op jit(solution)/shard_map/pallas_call | solution.py:533
  (140 shorter events, 37.9 us)
Async XLA Ops:
  13.0 15.9 %collective-permute-start.4 = (bf16[1552,128]{1,0:T(8,128)(2,1)}, bf16[1552,128]{1,0:T(8,128)(2,1)S(1)}, u32[]{:S(2)}, u32[]{:S(2)}) collective-permute-start(bf16[1552,128]{1,0:T(8,128)(2,1)} %get-tuple-element.26), channel_id=1, source_target_pairs={{0,2},{2,0},{4,6},{6,4},{8,10},{10,8},{12,14},{14,12},{1,3},{3,1},... | collective-permute-start | bytes 1191944 | tf_op jit(solution)/shard_map/ppermute | solution.py:380
  16.0 28.4 %collective-permute-start.5 = (bf16[1552,128]{1,0:T(8,128)(2,1)}, bf16[1552,128]{1,0:T(8,128)(2,1)S(1)}, u32[]{:S(2)}, u32[]{:S(2)}) collective-permute-start(bf16[1552,128]{1,0:T(8,128)(2,1)} %get-tuple-element.27), channel_id=1, source_target_pairs={{0,4},{2,6},{4,0},{6,2},{8,12},{10,14},{12,8},{14,10},{1,5},{3,7},... | collective-permute-start | bytes 1191944 | tf_op jit(solution)/shard_map/ppermute | solution.py:380
  17.6 33.1 %collective-permute-start.6 = (bf16[1552,128]{1,0:T(8,128)(2,1)}, bf16[1552,128]{1,0:T(8,128)(2,1)S(1)}, u32[]{:S(2)}, u32[]{:S(2)}) collective-permute-start(bf16[1552,128]{1,0:T(8,128)(2,1)} %get-tuple-element.28), channel_id=1, source_target_pairs={{0,6},{2,4},{4,2},{6,0},{8,14},{10,12},{12,10},{14,8},{1,7},{3,5},... | collective-permute-start | bytes 1191944 | tf_op jit(solution)/shard_map/ppermute | solution.py:380
  17.6 47.3 %collective-permute-start.2 = (bf16[1552,128]{1,0:T(8,128)(2,1)}, bf16[1552,128]{1,0:T(8,128)(2,1)S(1)}, u32[]{:S(2)}, u32[]{:S(2)}) collective-permute-start(bf16[1552,128]{1,0:T(8,128)(2,1)} %get-tuple-element.24), channel_id=1, source_target_pairs={{0,8},{2,10},{4,12},{6,14},{8,0},{10,2},{12,4},{14,6},{1,9},{3,11}... | collective-permute-start | bytes 1191944 | tf_op jit(solution)/shard_map/ppermute | solution.py:380
  20.6 54.1 %collective-permute-start.3 = (bf16[1552,128]{1,0:T(8,128)(2,1)}, bf16[1552,128]{1,0:T(8,128)(2,1)S(1)}, u32[]{:S(2)}, u32[]{:S(2)}) collective-permute-start(bf16[1552,128]{1,0:T(8,128)(2,1)} %get-tuple-element.25), channel_id=1, source_target_pairs={{0,10},{2,8},{4,14},{6,12},{8,2},{10,0},{12,6},{14,4},{1,11},{3,9}... | collective-permute-start | bytes 1191944 | tf_op jit(solution)/shard_map/ppermute | solution.py:380
  29.0 56.0 %collective-permute-start.1 = (bf16[1552,128]{1,0:T(8,128)(2,1)S(1)}, bf16[1552,128]{1,0:T(8,128)(2,1)S(1)}, u32[]{:S(2)}, u32[]{:S(2)}) collective-permute-start(bf16[1552,128]{1,0:T(8,128)(2,1)S(1)} %copy-done.16), channel_id=1, source_target_pairs={{0,12},{2,14},{4,8},{6,10},{8,4},{10,6},{12,0},{14,2},{1,13},{3,15... | collective-permute-start | bytes 1191944 | tf_op jit(solution)/shard_map/ppermute | solution.py:380
  44.4 47.2 %collective-permute-start = (bf16[1552,128]{1,0:T(8,128)(2,1)S(1)}, bf16[1552,128]{1,0:T(8,128)(2,1)S(1)}, u32[]{:S(2)}, u32[]{:S(2)}) collective-permute-start(bf16[1552,128]{1,0:T(8,128)(2,1)S(1)} %get-tuple-element.22), channel_id=1, source_target_pairs={{0,14},{2,12},{4,10},{6,8},{8,6},{10,4},{12,2},{14,0},{1,15},{3,13... | collective-permute-start | bytes 1191944 | tf_op jit(solution)/shard_map/ppermute | solution.py:380
  101.2 6.3 %collective-permute-start.7 = (f32[8,16,2304]{2,1,0:T(8,128)}, f32[8,16,2304]{2,1,0:T(8,128)}, u32[]{:S(2)}, u32[]{:S(2)}) collective-permute-start(f32[8,16,2304]{2,1,0:T(8,128)} %get-tuple-element.31), channel_id=1, source_target_pairs={{0,1},{1,0},{2,3},{3,2},{4,5},{5,4},{6,7},{7,6},{8,9},{9,8},{10,11... | collective-permute-start | bytes 3538952 | tf_op jit(solution)/shard_map/ppermute | solution.py:469
  101.2 4.0 %collective-permute-start.12 = (f32[8,8,2304]{2,1,0:T(8,128)}, f32[8,8,2304]{2,1,0:T(8,128)}, u32[]{:S(2)}, u32[]{:S(2)}) collective-permute-start(f32[8,8,2304]{2,1,0:T(8,128)} %get-tuple-element.33), channel_id=1, source_target_pairs={{0,1},{1,0},{2,3},{3,2},{4,5},{5,4},{6,7},{7,6},{8,9},{9,8},{10,11... | collective-permute-start | bytes 1769480 | tf_op jit(solution)/shard_map/ppermute | solution.py:468
  106.6 16.4 %collective-permute-start.13 = (f32[4,8,2304]{2,1,0:T(8,128)S(1)}, f32[4,8,2304]{2,1,0:T(8,128)S(1)}, u32[]{:S(2)}, u32[]{:S(2)}) collective-permute-start(f32[4,8,2304]{2,1,0:T(8,128)S(1)} %slice.72), channel_id=1, source_target_pairs={{0,8},{2,10},{4,12},{6,14},{8,0},{10,2},{12,4},{14,6},{1,9},{3,11}... | collective-permute-start | bytes 884744 | tf_op jit(solution)/shard_map/ppermute | solution.py:380
  109.0 16.2 %collective-permute-start.10 = (f32[2,16,2304]{2,1,0:T(8,128)S(1)}, f32[2,16,2304]{2,1,0:T(8,128)S(1)}, u32[]{:S(2)}, u32[]{:S(2)}) collective-permute-start(f32[2,16,2304]{2,1,0:T(8,128)S(1)} %get-tuple-element.54), channel_id=1, source_target_pairs={{0,6},{2,4},{4,2},{6,0},{8,14},{10,12},{12,10},{14,8},{1,7},{3,5},... | collective-permute-start | bytes 884744 | tf_op jit(solution)/shard_map/ppermute | solution.py:380
  112.4 13.3 %collective-permute-start.8 = (f32[2,16,2304]{2,1,0:T(8,128)S(1)}, f32[2,16,2304]{2,1,0:T(8,128)S(1)}, u32[]{:S(2)}, u32[]{:S(2)}) collective-permute-start(f32[2,16,2304]{2,1,0:T(8,128)S(1)} %get-tuple-element.52), channel_id=1, source_target_pairs={{0,2},{2,0},{4,6},{6,4},{8,10},{10,8},{12,14},{14,12},{1,3},{3,1},... | collective-permute-start | bytes 884744 | tf_op jit(solution)/shard_map/ppermute | solution.py:380
  113.8 17.2 %collective-permute-start.9 = (f32[2,16,2304]{2,1,0:T(8,128)S(1)}, f32[2,16,2304]{2,1,0:T(8,128)S(1)}, u32[]{:S(2)}, u32[]{:S(2)}) collective-permute-start(f32[2,16,2304]{2,1,0:T(8,128)S(1)} %get-tuple-element.53), channel_id=1, source_target_pairs={{0,4},{2,6},{4,0},{6,2},{8,12},{10,14},{12,8},{14,10},{1,5},{3,7},... | collective-permute-start | bytes 884744 | tf_op jit(solution)/shard_map/ppermute | solution.py:380
  131.1 9.1 %collective-permute-start.11 = (f32[16,2304]{1,0:T(8,128)S(1)}, f32[16,2304]{1,0:T(8,128)S(1)}, u32[]{:S(2)}, u32[]{:S(2)}) collective-permute-start(f32[16,2304]{1,0:T(8,128)S(1)} %slice_bitcast_fusion.4), channel_id=1, source_target_pairs={{0,8},{2,10},{4,12},{6,14},{8,0},{10,2},{12,4},{14,6},{1,9},{3,11}... | collective-permute-start | bytes 442376 | tf_op jit(solution)/shard_map/ppermute | solution.py:380
  131.8 8.5 %collective-permute-start.14 = (f32[8,2304]{1,0:T(8,128)S(1)}, f32[8,2304]{1,0:T(8,128)S(1)}, u32[]{:S(2)}, u32[]{:S(2)}) collective-permute-start(f32[8,2304]{1,0:T(8,128)S(1)} %get-tuple-element.55), channel_id=1, source_target_pairs={{0,2},{2,0},{4,6},{6,4},{8,10},{10,8},{12,14},{14,12},{1,3},{3,1},... | collective-permute-start | bytes 221192 | tf_op jit(solution)/shard_map/ppermute | solution.py:380
  133.3 7.7 %collective-permute-start.15 = (f32[8,2304]{1,0:T(8,128)S(1)}, f32[8,2304]{1,0:T(8,128)S(1)}, u32[]{:S(2)}, u32[]{:S(2)}) collective-permute-start(f32[8,2304]{1,0:T(8,128)S(1)} %get-tuple-element.57), channel_id=1, source_target_pairs={{0,4},{2,6},{4,0},{6,2},{8,12},{10,14},{12,8},{14,10},{1,5},{3,7},... | collective-permute-start | bytes 221192 | tf_op jit(solution)/shard_map/ppermute | solution.py:380
  135.8 5.6 %collective-permute-start.16 = (f32[8,2304]{1,0:T(8,128)S(1)}, f32[8,2304]{1,0:T(8,128)S(1)}, u32[]{:S(2)}, u32[]{:S(2)}) collective-permute-start(f32[8,2304]{1,0:T(8,128)S(1)} %get-tuple-element.56), channel_id=1, source_target_pairs={{0,6},{2,4},{4,2},{6,0},{8,14},{10,12},{12,10},{14,8},{1,7},{3,5},... | collective-permute-start | bytes 221192 | tf_op jit(solution)/shard_map/ppermute | solution.py:380
  141.4 6.7 %collective-permute-start.20 = (bf16[24,2304]{1,0:T(8,128)(2,1)S(1)}, bf16[24,2304]{1,0:T(8,128)(2,1)S(1)}, u32[]{:S(2)}, u32[]{:S(2)}) collective-permute-start(bf16[24,2304]{1,0:T(8,128)(2,1)S(1)} %pad_maximum_fusion.1), channel_id=1, source_target_pairs={{0,8},{2,10},{4,12},{6,14},{8,0},{10,2},{12,4},{14,6},{1,9},{3,11}... | collective-permute-start | bytes 331784 | tf_op jit(solution)/shard_map/ppermute | solution.py:380
  141.8 7.6 %collective-permute-start.17 = (bf16[24,2304]{1,0:T(8,128)(2,1)S(1)}, bf16[24,2304]{1,0:T(8,128)(2,1)S(1)}, u32[]{:S(2)}, u32[]{:S(2)}) collective-permute-start(bf16[24,2304]{1,0:T(8,128)(2,1)S(1)} %pad_maximum_fusion.1), channel_id=1, source_target_pairs={{0,2},{2,0},{4,6},{6,4},{8,10},{10,8},{12,14},{14,12},{1,3},{3,1},... | collective-permute-start | bytes 331784 | tf_op jit(solution)/shard_map/ppermute | solution.py:380
  143.4 9.1 %collective-permute-start.18 = (bf16[24,2304]{1,0:T(8,128)(2,1)S(1)}, bf16[24,2304]{1,0:T(8,128)(2,1)S(1)}, u32[]{:S(2)}, u32[]{:S(2)}) collective-permute-start(bf16[24,2304]{1,0:T(8,128)(2,1)S(1)} %pad_maximum_fusion.1), channel_id=1, source_target_pairs={{0,4},{2,6},{4,0},{6,2},{8,12},{10,14},{12,8},{14,10},{1,5},{3,7},... | collective-permute-start | bytes 331784 | tf_op jit(solution)/shard_map/ppermute | solution.py:380
  145.7 7.1 %collective-permute-start.19 = (bf16[24,2304]{1,0:T(8,128)(2,1)S(1)}, bf16[24,2304]{1,0:T(8,128)(2,1)S(1)}, u32[]{:S(2)}, u32[]{:S(2)}) collective-permute-start(bf16[24,2304]{1,0:T(8,128)(2,1)S(1)} %pad_maximum_fusion.1), channel_id=1, source_target_pairs={{0,6},{2,4},{4,2},{6,0},{8,14},{10,12},{12,10},{14,8},{1,7},{3,5},... | collective-permute-start | bytes 331784 | tf_op jit(solution)/shard_map/ppermute | solution.py:380
  148.1 6.5 %collective-permute-start.21 = (bf16[24,2304]{1,0:T(8,128)(2,1)S(1)}, bf16[24,2304]{1,0:T(8,128)(2,1)S(1)}, u32[]{:S(2)}, u32[]{:S(2)}) collective-permute-start(bf16[24,2304]{1,0:T(8,128)(2,1)S(1)} %collective-permute-done.20), channel_id=1, source_target_pairs={{0,2},{2,0},{4,6},{6,4},{8,10},{10,8},{12,14},{14,12},{1,3},{3,1},... | collective-permute-start | bytes 331784 | tf_op jit(solution)/shard_map/ppermute | solution.py:380
  149.4 5.7 %collective-permute-start.22 = (bf16[24,2304]{1,0:T(8,128)(2,1)S(1)}, bf16[24,2304]{1,0:T(8,128)(2,1)S(1)}, u32[]{:S(2)}, u32[]{:S(2)}) collective-permute-start(bf16[24,2304]{1,0:T(8,128)(2,1)S(1)} %collective-permute-done.20), channel_id=1, source_target_pairs={{0,4},{2,6},{4,0},{6,2},{8,12},{10,14},{12,8},{14,10},{1,5},{3,7},... | collective-permute-start | bytes 331784 | tf_op jit(solution)/shard_map/ppermute | solution.py:380
  149.4 7.3 %collective-permute-start.23 = (bf16[24,2304]{1,0:T(8,128)(2,1)S(1)}, bf16[24,2304]{1,0:T(8,128)(2,1)S(1)}, u32[]{:S(2)}, u32[]{:S(2)}) collective-permute-start(bf16[24,2304]{1,0:T(8,128)(2,1)S(1)} %collective-permute-done.20), channel_id=1, source_target_pairs={{0,6},{2,4},{4,2},{6,0},{8,14},{10,12},{12,10},{14,8},{1,7},{3,5},... | collective-permute-start | bytes 331784 | tf_op jit(solution)/shard_map/ppermute | solution.py:380
  156.7 2.5 collective-permute-start.24
  176.2 33.0 %collective-permute-start.30 = (bf16[1536,128]{1,0:T(8,128)(2,1)S(1)}, bf16[1536,128]{1,0:T(8,128)(2,1)S(1)}, u32[]{:S(2)}, u32[]{:S(2)}) collective-permute-start(bf16[1536,128]{1,0:T(8,128)(2,1)S(1)} %get-tuple-element.40), channel_id=1, source_target_pairs={{0,12},{2,14},{4,8},{6,10},{8,4},{10,6},{12,0},{14,2},{1,13},{3,15... | collective-permute-start | bytes 1179656 | tf_op jit(solution)/shard_map/ppermute | solution.py:380
  178.5 36.5 %collective-permute-start.31 = (bf16[1536,128]{1,0:T(8,128)(2,1)S(1)}, bf16[1536,128]{1,0:T(8,128)(2,1)S(1)}, u32[]{:S(2)}, u32[]{:S(2)}) collective-permute-start(bf16[1536,128]{1,0:T(8,128)(2,1)S(1)} %get-tuple-element.41), channel_id=1, source_target_pairs={{0,14},{2,12},{4,10},{6,8},{8,6},{10,4},{12,2},{14,0},{1,15},{3,13... | collective-permute-start | bytes 1179656 | tf_op jit(solution)/shard_map/ppermute | solution.py:380
  186.6 55.9 %collective-permute-start.29 = (bf16[1536,128]{1,0:T(8,128)(2,1)S(1)}, bf16[1536,128]{1,0:T(8,128)(2,1)}, u32[]{:S(2)}, u32[]{:S(2)}) collective-permute-start(bf16[1536,128]{1,0:T(8,128)(2,1)S(1)} %shard_map.175), channel_id=1, source_target_pairs={{0,10},{2,8},{4,14},{6,12},{8,2},{10,0},{12,6},{14,4},{1,11},{3,9}... | collective-permute-start | bytes 1179656 | tf_op jit(solution)/shard_map/ppermute | solution.py:380
  205.1 37.5 %collective-permute-start.25 = (bf16[1536,128]{1,0:T(8,128)(2,1)S(1)}, bf16[1536,128]{1,0:T(8,128)(2,1)S(1)}, u32[]{:S(2)}, u32[]{:S(2)}) collective-permute-start(bf16[1536,128]{1,0:T(8,128)(2,1)S(1)} %get-tuple-element.36), channel_id=1, source_target_pairs={{0,2},{2,0},{4,6},{6,4},{8,10},{10,8},{12,14},{14,12},{1,3},{3,1},... | collective-permute-start | bytes 1179656 | tf_op jit(solution)/shard_map/ppermute | solution.py:380
  207.0 35.5 %collective-permute-start.26 = (bf16[1536,128]{1,0:T(8,128)(2,1)}, bf16[1536,128]{1,0:T(8,128)(2,1)S(1)}, u32[]{:S(2)}, u32[]{:S(2)}) collective-permute-start(bf16[1536,128]{1,0:T(8,128)(2,1)} %get-tuple-element.37), channel_id=1, source_target_pairs={{0,4},{2,6},{4,0},{6,2},{8,12},{10,14},{12,8},{14,10},{1,5},{3,7},... | collective-permute-start | bytes 1179656 | tf_op jit(solution)/shard_map/ppermute | solution.py:380
  209.2 33.3 %collective-permute-start.27 = (bf16[1536,128]{1,0:T(8,128)(2,1)}, bf16[1536,128]{1,0:T(8,128)(2,1)S(1)}, u32[]{:S(2)}, u32[]{:S(2)}) collective-permute-start(bf16[1536,128]{1,0:T(8,128)(2,1)} %get-tuple-element.38), channel_id=1, source_target_pairs={{0,6},{2,4},{4,2},{6,0},{8,14},{10,12},{12,10},{14,8},{1,7},{3,5},... | collective-permute-start | bytes 1179656 | tf_op jit(solution)/shard_map/ppermute | solution.py:380
  215.0 32.9 %collective-permute-start.28 = (bf16[1536,128]{1,0:T(8,128)(2,1)S(1)}, bf16[1536,128]{1,0:T(8,128)(2,1)S(1)}, u32[]{:S(2)}, u32[]{:S(2)}) collective-permute-start(bf16[1536,128]{1,0:T(8,128)(2,1)S(1)} %get-tuple-element.39), channel_id=1, source_target_pairs={{0,8},{2,10},{4,12},{6,14},{8,0},{10,2},{12,4},{14,6},{1,9},{3,11}... | collective-permute-start | bytes 1179656 | tf_op jit(solution)/shard_map/ppermute | solution.py:380
  (25 other events, 264.6 us)
